TPU v7x, 128 devices: a whole 4x4x4 slice. The times are simulated.
128 devices in a mesh: gx: 8 (over y, z_hi), gy: 16 (over x, z_lo, core).
Axes of the slice: x: 4, y: 4, z: 4 (z_hi: 2, z_lo: 2; z = z_hi * 2 + z_lo), core: 2. Of those that a mesh axis runs over, the one named last changes fastest.
Arguments:
- q_nodes: bfloat16 [128, 512, 4096], P(('gx', 'gy')), may hold values from -30 to 30, as said below
- k_cache: bfloat16 [128, 1024, 512], P(('gx', 'gy')), may hold values from -6 to 6, as said below
- v_cache: bfloat16 [128, 1024, 512], P(('gx', 'gy')), may hold values from -6 to 6
- k_tree: bfloat16 [128, 512, 512], P(('gx', 'gy')), may hold values from -6 to 6
- v_tree: bfloat16 [128, 512, 512], P(('gx', 'gy')), may hold values from -6 to 6
- anc_bits: int32 [128, 512, 16], P(('gx', 'gy')), may hold values from -2147483648 to 2147483647, as said below
- node_count: int32 [128], P(('gx', 'gy')), may hold values from 1 to 512, as said below
- cache_len: int32 [128], P(('gx', 'gy')), may hold values from 256 to 1024, as said below
- sinks: float32 [64], replicated, may hold values from 5 to 10
- o_weight: bfloat16 [4096, 2880], P(('gx', 'gy')), may hold values from -0.09375 to 0.09375
Outputs:
- attended: bfloat16 [128, 512, 4096], P(('gx', 'gy'))
- projected: bfloat16 [128, 512, 2880], P(('gx', 'gy'))
Inputs may be any that keep to these rules, and one draw needn't show every extreme that they name: `q_nodes`: custom draw of queries. `k_cache`: custom draw of keys. `anc_bits`: bit j mod 32 of word j // 32 in row i is set exactly when tree node j is node i or one of its ancestors; node 0 is the root and a node's ancestors have lower indices. `node_count`: write request r as a * 16 + b with b < 16. Where a + b is even, the tree has more than (2) * 128 nodes; elsewhere it has at most 128. Request 0 has 512 nodes. `cache_len`: request 0 has 1024 cached positions.
All inputs are finite; a program needn't handle non-finite values.
Results may differ from a plain program's by a relative error of at most 0.0055.
Values may be sent and summed in bfloat16 or wider, within the bound.
A program may use at most 192 MiB of HBM per device.

v0:
```python
import jax
import jax.numpy as jnp
from jax import lax
from jax.sharding import PartitionSpec as P

QH = 64
KVH = 8
HD = 64
BLK = 128


MASKED = -1e30


def passed_along(x, axis, by):
    length = lax.axis_size(axis)
    return lax.ppermute(x, axis, [(i, (i + by) % length) for i in range(length)])


def unpack_bits(bit_words):
    shift_ids = jnp.arange(32, dtype=jnp.int32)
    bit_flags = jnp.bitwise_and(jnp.right_shift(bit_words[:, :, None], shift_ids), 1)
    return bit_flags.reshape(bit_words.shape[0], bit_words.shape[1] * 32) > 0


def attend_rows(
    q_rows, tree_ok, cache_keys, cache_values, tree_keys, tree_values, cache_count, sinks
):
    row_total = q_rows.shape[0]
    groups = QH // KVH
    head_width = groups * HD
    scale_factor = HD ** (-0.5)
    cache_ok = jnp.arange(cache_keys.shape[0], dtype=jnp.int32) < cache_count
    tree_mask = jnp.repeat(tree_ok, groups, axis=0)

    def per_kv_head(kv_head):
        q_part = lax.dynamic_slice_in_dim(q_rows, kv_head * head_width, head_width, 1).reshape(
            row_total * groups, HD
        )
        key_cache = lax.dynamic_slice_in_dim(cache_keys, kv_head * HD, HD, 1)
        value_cache = lax.dynamic_slice_in_dim(cache_values, kv_head * HD, HD, 1)
        key_tree = lax.dynamic_slice_in_dim(tree_keys, kv_head * HD, HD, 1)
        value_tree = lax.dynamic_slice_in_dim(tree_values, kv_head * HD, HD, 1)
        score_cache = (
            jnp.dot(q_part, key_cache.T, preferred_element_type=jnp.float32) * scale_factor
        )
        score_cache = jnp.where(cache_ok[None, :], score_cache, MASKED)
        score_tree = jnp.dot(q_part, key_tree.T, preferred_element_type=jnp.float32) * scale_factor
        score_tree = jnp.where(tree_mask, score_tree, MASKED)
        sink_rows = jnp.tile(
            lax.dynamic_slice_in_dim(sinks, kv_head * groups, groups, 0), row_total
        )
        row_max = jnp.maximum(
            sink_rows, jnp.maximum(jnp.max(score_cache, axis=1), jnp.max(score_tree, axis=1))
        )
        weight_cache = jnp.exp(score_cache - row_max[:, None])
        weight_tree = jnp.exp(score_tree - row_max[:, None])
        denominator = (
            jnp.exp(sink_rows - row_max)
            + jnp.sum(weight_cache, axis=1)
            + jnp.sum(weight_tree, axis=1)
        )
        numerator = jnp.dot(
            weight_cache.astype(jnp.bfloat16), value_cache, preferred_element_type=jnp.float32
        )
        numerator = numerator + jnp.dot(
            weight_tree.astype(jnp.bfloat16), value_tree, preferred_element_type=jnp.float32
        )
        return (numerator / denominator[:, None]).reshape(row_total, head_width)

    per_head = lax.map(per_kv_head, jnp.arange(KVH, dtype=jnp.int32))
    return jnp.transpose(per_head, (1, 0, 2)).reshape(row_total, QH * HD)


def on_device(
    q_nodes, k_cache, v_cache, k_tree, v_tree, anc_bits, node_count, cache_len, sinks, o_weight
):
    queries = q_nodes[0]
    cache_keys = k_cache[0]
    cache_values = v_cache[0]
    tree_keys = k_tree[0]
    tree_values = v_tree[0]
    bit_words = anc_bits[0]
    node_limit = node_count[0]
    cache_count = cache_len[0]
    node_total = queries.shape[0]
    block_size = BLK
    block_count = node_total // block_size
    live_blocks = (node_limit + block_size - 1) // block_size

    def home_step(block_index, result):
        row_start = block_index * block_size
        q_rows = lax.dynamic_slice_in_dim(queries, row_start, block_size, 0)
        bit_rows = lax.dynamic_slice_in_dim(bit_words, row_start, block_size, 0)
        rows_out = attend_rows(
            q_rows,
            unpack_bits(bit_rows),
            cache_keys,
            cache_values,
            tree_keys,
            tree_values,
            cache_count,
            sinks,
        )
        return lax.dynamic_update_slice_in_dim(result, rows_out.astype(jnp.bfloat16), row_start, 0)

    result = jnp.zeros_like(queries)
    send_x = (live_blocks >= block_count - 1).astype(jnp.int32)
    send_y = (live_blocks >= block_count).astype(jnp.int32)
    kept_blocks = live_blocks - send_x - send_y
    start_x = jnp.minimum(kept_blocks, block_count - 1) * block_size
    start_y = jnp.minimum(kept_blocks + send_x, block_count - 1) * block_size
    tree_rows_x = (block_count - 1) * block_size

    def make_parcel(row_start, is_moved, tree_rows):
        q_rows = lax.dynamic_slice_in_dim(queries, row_start, block_size, 0)
        bit_rows = lax.dynamic_slice_in_dim(bit_words, row_start, block_size, 0)
        header = jnp.stack([is_moved, cache_count])
        return (
            q_rows,
            bit_rows,
            cache_keys,
            cache_values,
            tree_keys[:tree_rows],
            tree_values[:tree_rows],
            header,
        )

    def attend_moved(parcel):
        q_rows, bit_rows, moved_keys, moved_values, moved_tree_keys, moved_tree_values, header = (
            parcel
        )

        def compute_block():
            tree_ok = unpack_bits(bit_rows)[:, : moved_tree_keys.shape[0]]
            return attend_rows(
                q_rows,
                tree_ok,
                moved_keys,
                moved_values,
                moved_tree_keys,
                moved_tree_values,
                header[1],
                sinks,
            ).astype(jnp.bfloat16)

        def empty_block():
            return jnp.zeros((block_size, QH * HD), jnp.bfloat16)

        return lax.cond(header[0] > 0, compute_block, empty_block)

    def put_back(result, rows_out, row_start, is_moved):
        current = lax.dynamic_slice_in_dim(result, row_start, block_size, 0)
        chosen_rows = jnp.where(is_moved > 0, rows_out, current)
        return lax.dynamic_update_slice_in_dim(result, chosen_rows, row_start, 0)

    parcel_x = make_parcel(start_x, send_x, tree_rows_x)
    parcel_y = make_parcel(start_y, send_y, node_total)
    got_x = passed_along(
        (parcel_x[0], parcel_x[1], parcel_x[2], parcel_x[3], parcel_x[4], parcel_x[5], parcel_x[6]),
        "gx",
        1,
    )
    got_y = passed_along(
        (parcel_y[0], parcel_y[1], parcel_y[2], parcel_y[3], parcel_y[4], parcel_y[5], parcel_y[6]),
        "gy",
        1,
    )
    result = lax.fori_loop(0, kept_blocks, home_step, result)
    done_x = attend_moved(got_x)
    done_y = attend_moved(got_y)
    returned_x = passed_along(done_x, "gx", -1)
    returned_y = passed_along(done_y, "gy", -1)
    result = put_back(result, returned_x, start_x, send_x)
    result = put_back(result, returned_y, start_y, send_y)
    node_live = jnp.arange(node_total, dtype=jnp.int32) < node_limit
    attended = jnp.where(node_live[:, None], result, jnp.zeros_like(result))
    projected = jnp.dot(
        attended,
        lax.all_gather(o_weight, ("gx", "gy"), axis=0, tiled=True),
        preferred_element_type=jnp.float32,
    )
    return (attended[None], projected.astype(jnp.bfloat16)[None])


def solution(mesh):
    placed = (
        P(("gx", "gy"), None, None),
        P(("gx", "gy"), None, None),
        P(("gx", "gy"), None, None),
        P(("gx", "gy"), None, None),
        P(("gx", "gy"), None, None),
        P(("gx", "gy"), None, None),
        P(("gx", "gy")),
        P(("gx", "gy")),
        P(),
        P(("gx", "gy"), None),
    )
    return jax.shard_map(
        on_device,
        mesh=mesh,
        in_specs=placed,
        out_specs=(P(("gx", "gy"), None, None), P(("gx", "gy"), None, None)),
        check_vma=False,
    )
```

profile of v0, /device:TPU:1, one launch (start us, length us, event | category | flops | bytes accessed | tf_op | source)
XLA Modules:
  0.0 616.6 jit_solution(16396618629432415991)
XLA Ops:
  10.7 4.4 collective-permute-start.2
  15.5 3.5 collective-permute-start.5
  21.3 3.6 collective-permute-start
  24.8 68.9 %collective-permute-done = s32[2]{0:T(128)S(1)} collective-permute-done((s32[2]{0:T(128)S(1)}, s32[2]{0:T(128)S(1)}, u32[]{:S(2)}, u32[]{:S(2)}) %collective-permute-start) | collective-permute-done | bytes 40 | tf_op jit(solution)/shard_map/ppermute | solution.py:17
  94.0 5.9 collective-permute-done.1
  104.1 16.4 %collective-permute-done.6 = bf16[384,512]{1,0:T(8,128)(2,1)} collective-permute-done((bf16[384,512]{1,0:T(8,128)(2,1)S(1)}, bf16[384,512]{1,0:T(8,128)(2,1)}, u32[]{:S(2)}, u32[]{:S(2)}) %collective-permute-start.6) | collective-permute-done | bytes 393248 | tf_op jit(solution)/shard_map/ppermute | solution.py:17
  122.0 142.2 %conditional.2 = (bf16[128,4096]{1,0:T(8,128)(2,1)}) conditional(s32[]{:T(128)} %bitcast.17, () %tuple.37, (s32[2]{0:T(128)S(1)}, s32[128,16]{0,1:T(8,128)S(1)}, bf16[128,4096]{1,0:T(8,128)(2,1)}, bf16[1024,512]{1,0:T(8,128)(2,1)S(1)}, f32[64]{0:T(128)S(1)}, /*index=5*/bf16[384,512]{1,0:T(8,128)(2,1)}, bf16[1024,512]{1,0:T(8,128)(2,1)}, ...), branch_computations={%region_8.9_spmd, %region_9.16_spmd} | conditional | flops 383731712 | bytes 41591464 | solution.py:150
  123.0 138.8 %while.41 = (s32[]{:T(128)}, bf16[8,128,512]{2,1,0:T(8,128)(2,1)}, s32[8]{0:T(128)S(1)}, bf16[128,4096]{1,0:T(8,128)(2,1)}, bf16[1024,512]{1,0:T(8,128)(2,1)S(1)...) while((s32[]{:T(128)}, bf16[8,128,512]{2,1,0:T(8,128)(2,1)}, ...), condition=%wide.region_15.15_spmd.clone, body=%wide.region_10.14_spmd.clone.sunk | while | flops 383584256 | bytes 38872024 | solution.py:71
  149.6 3.3 fusion.169
  167.0 3.3 fusion.169
  184.3 3.3 fusion.169
  201.7 3.3 fusion.169
  219.0 3.3 fusion.169
  236.4 3.3 fusion.169
  253.8 3.3 fusion.169
  265.2 3.5 collective-permute-start.7
  271.3 147.5 %while.44 = (s32[]{:T(128)}, bf16[512,4096]{1,0:T(8,128)(2,1)}, s32[]{:T(128)}, bf16[512,4096]{1,0:T(8,128)(2,1)}, s32[]{:T(128)}, /*index=5*/s32[512,16]{0,1:T(...) while((s32[]{:T(128)}, bf16[512,4096]{1,0:T(8,128)(2,1)}, ...), condition=%wide.region_7.8_spmd, body=%wide.region_0.7_spmd.sunk | while | flops 418252800 | bytes 47441316 | solution.py:169
  273.2 143.1 %while.45 = (s32[]{:T(128)}, bf16[8,128,512]{2,1,0:T(8,128)(2,1)}, s32[8]{0:T(128)S(1)}, bf16[128,4096]{1,0:T(8,128)(2,1)S(1)}, bf16[1024,512]{1,0:T(8,128)(2,1)...) while((s32[]{:T(128)}, bf16[8,128,512]{2,1,0:T(8,128)(2,1)}, ...), condition=%wide.region_6.6_spmd.clone, body=%wide.region_1.5_spmd.clone.sunk | while | flops 418056192 | bytes 40920024 | solution.py:71
  276.0 3.7 fusion.141
  293.9 3.7 fusion.141
  311.8 3.7 fusion.141
  318.7 3.3 fusion.145
  329.7 3.7 fusion.141
  336.6 3.3 fusion.145
  347.6 3.7 fusion.141
  354.6 3.3 fusion.145
  365.5 3.7 fusion.141
  372.4 3.3 fusion.145
  383.4 3.7 fusion.141
  390.3 3.2 fusion.145
  401.3 3.7 fusion.141
  408.2 3.2 fusion.145
  419.5 149.3 %conditional.3 = (bf16[128,4096]{1,0:T(8,128)(2,1)S(1)}) conditional(s32[]{:T(128)} %bitcast.23, () %tuple.39, (s32[2]{0:T(128)}, s32[128,16]{0,1:T(8,128)}, bf16[128,4096]{1,0:T(8,128)(2,1)}, bf16[1024,512]{1,0:T(8,128)(2,1)}, f32[64]{0:T(128)S(1)}, /*index=5*/bf16[512,512]{1,0:T(8,128)(2,1)}, bf16[1024,512]{1,0:T(8,128)(2,1)}, ...), branch_computations={%region_16.17_spmd, %region_17.24_spmd} | conditional | flops 418252800 | bytes 43229868 | solution.py:150
  421.9 146.7 %while.42 = (s32[]{:T(128)}, bf16[8,128,512]{2,1,0:T(8,128)(2,1)S(1)}, s32[8]{0:T(128)S(1)}, bf16[128,4096]{1,0:T(8,128)(2,1)}, bf16[1024,512]{1,0:T(8,128)(2,1)...) while((s32[]{:T(128)}, ...), condition=%wide.region_23.23_spmd.clone, body=%wide.region_18.22_spmd.clone.sunk | while | flops 418056192 | bytes 40919516 | solution.py:71
  425.7 3.7 fusion.153
  432.7 3.2 fusion.157
  444.1 3.7 fusion.153
  462.4 3.7 fusion.153
  469.4 3.2 fusion.157
  480.7 3.7 fusion.153
  499.1 3.7 fusion.153
  506.1 3.2 fusion.157
  517.4 3.7 fusion.153
  535.8 3.7 fusion.153
  554.1 3.7 fusion.153
  571.6 11.7 %collective-permute-done.15 = bf16[128,4096]{1,0:T(8,128)(2,1)S(1)} collective-permute-done((bf16[128,4096]{1,0:T(8,128)(2,1)S(1)}, bf16[128,4096]{1,0:T(8,128)(2,1)S(1)}, u32[]{:S(2)}, u32[]{:S(2)}) %collective-permute-start.15) | collective-permute-done | bytes 1048608 | tf_op jit(solution)/shard_map/ppermute | solution.py:17
  585.8 4.5 fusion.85
  590.4 19.4 %fusion.84 = bf16[1,512,2880]{1,2,0:T(8,128)(2,1)} fusion(bf16[4096,2880]{1,0:T(8,128)(2,1)} %all-gather.2.cloned.1.call-done, bf16[512,4096]{1,0:T(8,128)(2,1)} %select_dynamic-update-slice_fusion, pred[512]{0:T(512)(128)(4,1)S(1)} %iota_compare_fusion.3), kind=kOutput, calls=%fused_computation.116 | convolution fusion | flops 12083167232 | bytes 30736896 | tf_op jit(solution)/shard_map/dot_general | solution.py:178
  (570 shorter events, 296.8 us)
Async XLA Ops:
  7.2 17.7 %copy-start.4 = (s32[1,512,16]{1,2,0:T(8,128)S(1)}, s32[1,512,16]{1,2,0:T(8,128)}, u32[]{:S(2)}) copy-start(s32[1,512,16]{1,2,0:T(8,128)} %param.27) | copy-start | bytes 98308
  7.2 114.8 %copy-start.6 = (f32[64]{0:T(128)S(1)}, f32[64]{0:T(128)}, u32[]{:S(2)}) copy-start(f32[64]{0:T(128)} %param.30) | copy-start | bytes 772
  7.2 583.2 %all-gather.2.cloned.1.call-start = ((), (), s32[]{:S(2)}) async-start(), calls=%async_computation | async-start | bytes 24305664 | tf_op jit(solution)/shard_map/all_gather | solution.py:180
  10.7 110.0 %collective-permute-start.2 = (bf16[128,4096]{1,0:T(8,128)(2,1)S(1)}, bf16[128,4096]{1,0:T(8,128)(2,1)}, u32[]{:S(2)}, u32[]{:S(2)}) collective-permute-start(bf16[128,4096]{1,0:T(8,128)(2,1)S(1)} %get-tuple-element.501), channel_id=1, source_target_pairs={{0,16},{16,32},{32,48},{48,64},{64,80},{80,96},{96,112},{112,0},{1... | collective-permute-start | bytes 3145736 | tf_op jit(solution)/shard_map/ppermute | solution.py:17
  15.0 106.7 %collective-permute-start.3 = (bf16[1024,512]{1,0:T(8,128)(2,1)}, bf16[1024,512]{1,0:T(8,128)(2,1)S(1)}, u32[]{:S(2)}, u32[]{:S(2)}) collective-permute-start(bf16[1024,512]{1,0:T(8,128)(2,1)} %bitcast.12), channel_id=1, source_target_pairs={{0,16},{16,32},{32,48},{48,64},{64,80},{80,96},{96,112},{112,0},{1... | collective-permute-start | bytes 3145736 | tf_op jit(solution)/shard_map/ppermute | solution.py:17
  15.5 106.4 %collective-permute-start.5 = (bf16[1024,512]{1,0:T(8,128)(2,1)}, bf16[1024,512]{1,0:T(8,128)(2,1)}, u32[]{:S(2)}, u32[]{:S(2)}) collective-permute-start(bf16[1024,512]{1,0:T(8,128)(2,1)} %bitcast.14), channel_id=1, source_target_pairs={{0,16},{16,32},{32,48},{48,64},{64,80},{80,96},{96,112},{112,0},{1... | collective-permute-start | bytes 3145736 | tf_op jit(solution)/shard_map/ppermute | solution.py:17
  20.0 83.9 %collective-permute-start.4 = (bf16[384,512]{1,0:T(8,128)(2,1)S(1)}, bf16[384,512]{1,0:T(8,128)(2,1)}, u32[]{:S(2)}, u32[]{:S(2)}) collective-permute-start(bf16[384,512]{1,0:T(8,128)(2,1)S(1)} %slice_bitcast_fusion.1), channel_id=1, source_target_pairs={{0,16},{16,32},{32,48},{48,64},{64,80},{80,96},{96,112},{112,0},{1... | collective-permute-start | bytes 1179656 | tf_op jit(solution)/shard_map/ppermute | solution.py:17
  21.3 72.5 %collective-permute-start = (s32[2]{0:T(128)S(1)}, s32[2]{0:T(128)S(1)}, u32[]{:S(2)}, u32[]{:S(2)}) collective-permute-start(s32[2]{0:T(128)S(1)} %pad_add_fusion), channel_id=1, source_target_pairs={{0,16},{16,32},{32,48},{48,64},{64,80},{80,96},{96,112},{112,0},{1... | collective-permute-start | bytes 32 | tf_op jit(solution)/shard_map/ppermute | solution.py:17
  93.8 6.1 collective-permute-start.1
  99.9 165.3 %collective-permute-start.12 = (bf16[512,512]{1,0:T(8,128)(2,1)}, bf16[512,512]{1,0:T(8,128)(2,1)S(1)}, u32[]{:S(2)}, u32[]{:S(2)}) collective-permute-start(bf16[512,512]{1,0:T(8,128)(2,1)} %bitcast.13), channel_id=1, source_target_pairs={{0,1},{1,2},{2,3},{3,4},{4,5},{5,6},{6,7},{7,8},{8,9},{9,10},{10,1... | collective-permute-start | bytes 1572872 | tf_op jit(solution)/shard_map/ppermute | solution.py:17
  104.0 16.5 %collective-permute-start.6 = (bf16[384,512]{1,0:T(8,128)(2,1)S(1)}, bf16[384,512]{1,0:T(8,128)(2,1)}, u32[]{:S(2)}, u32[]{:S(2)}) collective-permute-start(bf16[384,512]{1,0:T(8,128)(2,1)S(1)} %slice_bitcast_fusion), channel_id=1, source_target_pairs={{0,16},{16,32},{32,48},{48,64},{64,80},{80,96},{96,112},{112,0},{1... | collective-permute-start | bytes 1179656 | tf_op jit(solution)/shard_map/ppermute | solution.py:17
  120.5 143.7 %collective-permute-start.9 = (s32[128,16]{0,1:T(8,128)S(1)}, s32[128,16]{0,1:T(8,128)S(1)}, u32[]{:S(2)}, u32[]{:S(2)}) collective-permute-start(s32[128,16]{0,1:T(8,128)S(1)} %get-tuple-element.502), channel_id=1, source_target_pairs={{0,1},{1,2},{2,3},{3,4},{4,5},{5,6},{6,7},{7,8},{8,9},{9,10},{10,1... | collective-permute-start | bytes 24584 | tf_op jit(solution)/shard_map/ppermute | solution.py:17
  120.7 298.8 %collective-permute-start.11 = (bf16[1024,512]{1,0:T(8,128)(2,1)}, bf16[1024,512]{1,0:T(8,128)(2,1)}, u32[]{:S(2)}, u32[]{:S(2)}) collective-permute-start(bf16[1024,512]{1,0:T(8,128)(2,1)} %bitcast.12), channel_id=1, source_target_pairs={{0,1},{1,2},{2,3},{3,4},{4,5},{5,6},{6,7},{7,8},{8,9},{9,10},{10,1... | collective-permute-start | bytes 3145736 | tf_op jit(solution)/shard_map/ppermute | solution.py:17
  121.8 297.7 %collective-permute-start.13 = (bf16[1024,512]{1,0:T(8,128)(2,1)}, bf16[1024,512]{1,0:T(8,128)(2,1)}, u32[]{:S(2)}, u32[]{:S(2)}) collective-permute-start(bf16[1024,512]{1,0:T(8,128)(2,1)} %bitcast.14), channel_id=1, source_target_pairs={{0,1},{1,2},{2,3},{3,4},{4,5},{5,6},{6,7},{7,8},{8,9},{9,10},{10,1... | collective-permute-start | bytes 3145736 | tf_op jit(solution)/shard_map/ppermute | solution.py:17
  121.9 142.3 %collective-permute-start.8 = (s32[2]{0:T(128)S(1)}, s32[2]{0:T(128)S(1)}, u32[]{:S(2)}, u32[]{:S(2)}) collective-permute-start(s32[2]{0:T(128)S(1)} %pad_add_fusion.1), channel_id=1, source_target_pairs={{0,1},{1,2},{2,3},{3,4},{4,5},{5,6},{6,7},{7,8},{8,9},{9,10},{10,1... | collective-permute-start | bytes 32 | tf_op jit(solution)/shard_map/ppermute | solution.py:17
  132.3 3.5 copy-start.1
  149.6 3.6 copy-start.1
  166.9 3.6 copy-start.1
  184.3 3.6 copy-start.1
  201.6 3.6 copy-start.1
  219.0 3.6 copy-start.1
  236.4 3.6 copy-start.1
  253.7 3.6 copy-start.1
  264.2 7.1 %copy-start.7 = (s32[2]{0:T(128)}, s32[2]{0:T(128)S(1)}, u32[]{:S(2)}) copy-start(s32[2]{0:T(128)S(1)} %collective-permute-done.8) | copy-start | bytes 28
  264.2 155.2 %collective-permute-start.10 = (bf16[128,4096]{1,0:T(8,128)(2,1)}, bf16[128,4096]{1,0:T(8,128)(2,1)}, u32[]{:S(2)}, u32[]{:S(2)}) collective-permute-start(bf16[128,4096]{1,0:T(8,128)(2,1)} %get-tuple-element.500), channel_id=1, source_target_pairs={{0,1},{1,2},{2,3},{3,4},{4,5},{5,6},{6,7},{7,8},{8,9},{9,10},{10,1... | collective-permute-start | bytes 3145736 | tf_op jit(solution)/shard_map/ppermute | solution.py:17
  264.2 7.1 %copy-start.5 = (s32[128,16]{0,1:T(8,128)}, s32[128,16]{0,1:T(8,128)S(1)}, u32[]{:S(2)}) copy-start(s32[128,16]{0,1:T(8,128)S(1)} %collective-permute-done.9) | copy-start | bytes 24580
  264.2 155.2 %collective-permute-start.14 = (bf16[512,512]{1,0:T(8,128)(2,1)}, bf16[512,512]{1,0:T(8,128)(2,1)}, u32[]{:S(2)}, u32[]{:S(2)}) collective-permute-start(bf16[512,512]{1,0:T(8,128)(2,1)} %bitcast.15), channel_id=1, source_target_pairs={{0,1},{1,2},{2,3},{3,4},{4,5},{5,6},{6,7},{7,8},{8,9},{9,10},{10,1... | collective-permute-start | bytes 1572872 | tf_op jit(solution)/shard_map/ppermute | solution.py:17
  265.2 6.1 copy-start.3
  265.2 303.9 %collective-permute-start.7 = (bf16[128,4096]{1,0:T(8,128)(2,1)}, bf16[128,4096]{1,0:T(8,128)(2,1)}, u32[]{:S(2)}, u32[]{:S(2)}) collective-permute-start(bf16[128,4096]{1,0:T(8,128)(2,1)} %get-tuple-element.1062), channel_id=1, source_target_pairs={{0,112},{16,0},{32,16},{48,32},{64,48},{80,64},{96,80},{112,96},{1... | collective-permute-start | bytes 3145736 | tf_op jit(solution)/shard_map/ppermute | solution.py:17
  282.9 3.6 copy-start
  300.8 3.6 copy-start
  318.7 3.7 copy-start
  336.6 3.7 copy-start
  354.5 3.6 copy-start
  372.4 3.6 copy-start
  390.3 3.6 copy-start
  408.2 3.6 copy-start
  432.7 3.6 copy-start.2
  451.0 3.6 copy-start.2
  469.4 3.6 copy-start.2
  487.7 3.6 copy-start.2
  506.0 3.6 copy-start.2
  524.4 3.6 copy-start.2
  542.7 3.6 copy-start.2
  561.1 3.6 copy-start.2
  568.8 14.5 %collective-permute-start.15 = (bf16[128,4096]{1,0:T(8,128)(2,1)S(1)}, bf16[128,4096]{1,0:T(8,128)(2,1)S(1)}, u32[]{:S(2)}, u32[]{:S(2)}) collective-permute-start(bf16[128,4096]{1,0:T(8,128)(2,1)S(1)} %get-tuple-element.1063), channel_id=1, source_target_pairs={{0,15},{1,0},{2,1},{3,2},{4,3},{5,4},{6,5},{7,6},{8,7},{9,8},{10,9... | collective-permute-start | bytes 3145736 | tf_op jit(solution)/shard_map/ppermute | solution.py:17
Sparse Core Ops, SparseCore 0:
  104.2 281.0 all-gather.1
where the time goes:
time: 621 us; the launch traced here: 617 us
  matrix products  220 us (35%)
  other arithmetic  112 us (18%)
  waiting for transfers between devices  103 us (17%)
  local copies, waits for them, and re-layouts  94.1 us (15%)
  loops' own time  49.7 us (8%)
  starting transfers between devices  21.9 us (4%)
  between operations  16.2 us (3%)
    ppermute x16, waiting for transfers between devices, passed_along(): lax.ppermute(x, axis, [(i, (i + by) % length) for i in range(length)])  103 us
    dot_general x24, matrix products, per_kv_head(): jnp.dot(q_part, key_cache.T, preferred_element_type=jnp.float32)  81.8 us
    reduce_sum x24, other arithmetic, per_kv_head(): jnp.sum(weight_cache, axis=1)  78.5 us
    dot_general x24, matrix products, per_kv_head(): jnp.dot(weight_cache.astype(jnp.bfloat16), value_cache, preferred_element...  51 us
    another operation x3, loops' own time, attend_rows(): per_head = lax.map(per_kv_head, jnp.arange(KVH, dtype=jnp.int32))  49.4 us
    dot_general x24, matrix products, per_kv_head(): jnp.dot(q_part, key_tree.T, preferred_element_type=jnp.float32)  34.5 us
    dot_general x24, matrix products, per_kv_head(): jnp.dot(weight_tree.astype(jnp.bfloat16), value_tree, preferred_element_t...  32.8 us
    ppermute x16, starting transfers between devices, passed_along(): lax.ppermute(x, axis, [(i, (i + by) % length) for i in range(length)])  21.9 us
  transfers between devices with their start and end apart: 17, of which 4 were waited for; matrix products, arithmetic and copies ran while one was open for 65% of the time, Pallas kernels for 0%

commit v1 on v0

v1 whole, which is shorter than its diff:
```python
import functools

import jax
import jax.numpy as jnp
from jax import lax
from jax.experimental import pallas as pl
from jax.experimental.pallas import tpu as pltpu
from jax.sharding import Mesh, PartitionSpec as P

HD = 64
NODES = 512
LIGHT = 128
CACHE = 1024
HALF = 2048
COLS = 1536
D = 2880
TILE = 256
SUMS = 16
EXP_SCALE = 0.125 * 1.4426950408889634
MASKED = -1.0e30
F32 = jnp.float32
BF16 = jnp.bfloat16


def lane_ids(shape):
    return lax.broadcasted_iota(jnp.int32, shape, len(shape) - 1)


def row_ids(shape):
    return lax.broadcasted_iota(jnp.int32, shape, len(shape) - 2)


def build_bias(bits_ref, bias_ref, keys, nodes):
    shift = row_ids((32, nodes))
    for word in range(keys // 32):
        row = jnp.broadcast_to(bits_ref[word : word + 1, :nodes], (32, nodes))
        bit = jnp.bitwise_and(lax.shift_right_logical(row, shift), 1)
        bias_ref[word * 32 : word * 32 + 32, :] = jnp.where(bit > 0, 0.0, MASKED)


def spread_keys(pair, second):
    wide = pair.astype(F32)
    turned = pltpu.roll(wide, HD, 1)
    take_own = (lane_ids(wide.shape) < HD) == jnp.logical_not(second)
    return jnp.where(take_own, wide, turned)


def turn_values(pair, second):
    turned = pair.astype(F32).T
    return jnp.where(second, turned[HD:], turned[:HD])


def prepare(k_cache, v_cache, k_tree, v_tree, length, second, keys_ref, values_ref, tree):
    keys = spread_keys(k_cache, second)
    keys_ref[pl.ds(0, CACHE), :] = jnp.where(row_ids(keys.shape) < length, keys, 0.0).astype(BF16)
    keys_ref[pl.ds(CACHE, tree), :] = spread_keys(k_tree, second).astype(BF16)
    values = turn_values(v_cache, second)
    live = lane_ids(values.shape) < length
    values_ref[pl.ds(0, HD), pl.ds(0, CACHE)] = jnp.where(live, values, 0.0).astype(BF16)
    live = lane_ids((SUMS, CACHE)) < length
    values_ref[pl.ds(HD, SUMS), pl.ds(0, CACHE)] = jnp.where(live, 1.0, 0.0).astype(BF16)
    values_ref[pl.ds(0, HD), pl.ds(CACHE, tree)] = turn_values(v_tree, second).astype(BF16)
    values_ref[pl.ds(HD, SUMS), pl.ds(CACHE, tree)] = jnp.ones((SUMS, tree), BF16)


def contract_last(a, b):
    return lax.dot_general(a, b, (((1,), (1,)), ((), ())), preferred_element_type=F32)


def attend_tile(keys_ref, values_ref, queries, bias, sink, tree, node_ok):
    cache_scores = contract_last(keys_ref[pl.ds(0, CACHE), :], queries)
    tree_scores = contract_last(keys_ref[pl.ds(CACHE, tree), :], queries) + bias
    row_max = jnp.maximum(
        jnp.max(cache_scores, axis=0, keepdims=True), jnp.max(tree_scores, axis=0, keepdims=True)
    )
    row_max = jnp.maximum(row_max, sink)
    cache_weights = jnp.exp2((cache_scores - row_max) * EXP_SCALE).astype(BF16)
    tree_weights = jnp.exp2((tree_scores - row_max) * EXP_SCALE).astype(BF16)
    sums = jnp.dot(values_ref[:, pl.ds(0, CACHE)], cache_weights, preferred_element_type=F32)
    sums += jnp.dot(values_ref[:, pl.ds(CACHE, tree)], tree_weights, preferred_element_type=F32)
    denominator = sums[HD : HD + 1] + jnp.exp2((sink - row_max) * EXP_SCALE)
    return sums[:HD] * jnp.where(node_ok, 1.0 / denominator, 0.0)


def attend_head_pair(pair, first_head, refs, counts):
    (q_busy, q_light, keys_b, values_b, keys_l, values_l, bias_b, bias_l, sinks, out_b, out_l) = refs
    count_b, count_l = counts
    lanes = pl.ds(pl.multiple_of(pair * 128, 128), 128)
    sink_even = sinks[first_head + 2 * pair] * 8.0
    sink_odd = sinks[first_head + 2 * pair + 1] * 8.0
    for tile in range(NODES // TILE):
        rows = pl.ds(tile * TILE, TILE)
        tree = (tile + 1) * TILE
        queries = q_busy[rows, lanes]
        left = lane_ids(queries.shape) < HD
        bias = bias_b[pl.ds(0, tree), rows]
        node_ok = lane_ids((1, TILE)) + tile * TILE < count_b
        zero = jnp.zeros_like(queries)
        even = attend_tile(
            keys_b, values_b, jnp.where(left, queries, zero), bias, sink_even, tree, node_ok
        )
        odd = attend_tile(
            keys_b, values_b, jnp.where(left, zero, queries), bias, sink_odd, tree, node_ok
        )
        out_b[rows, lanes] = jnp.concatenate([even, odd], axis=0).T.astype(BF16)
    queries = q_light[:, lanes]
    left = lane_ids(queries.shape) < HD
    zero = jnp.zeros_like(queries)
    both = jnp.concatenate([jnp.where(left, queries, zero), jnp.where(left, zero, queries)], axis=0)
    columns = lane_ids((1, TILE))
    sink = jnp.where(columns < LIGHT, sink_even, sink_odd)
    node_ok = jnp.where(columns < LIGHT, columns, columns - LIGHT) < count_l
    bias = jnp.concatenate([bias_l[...], bias_l[...]], axis=1)
    result = attend_tile(keys_l, values_l, both, bias, sink, LIGHT, node_ok)
    stacked = jnp.concatenate([result[:, :LIGHT], result[:, LIGHT:]], axis=0)
    out_l[:, lanes] = stacked.T.astype(BF16)


def attention_kernel(
    scalars, sinks, q_busy, q_light, kc_b, vc_b, kt_b, vt_b, kc_l, vc_l, kt_l, vt_l, bits_b, bits_l,
    out_b, out_l, keys_b, values_b, keys_l, values_l, bias_b, bias_l,
):
    build_bias(bits_b, bias_b, NODES, NODES)
    build_bias(bits_l, bias_l, LIGHT, LIGHT)
    head_base = scalars[4]
    refs = (q_busy, q_light, keys_b, values_b, keys_l, values_l, bias_b, bias_l, sinks, out_b, out_l)

    def per_kv(kv, carry):
        second = lax.rem(kv, 2) == 1
        lanes = pl.ds(pl.multiple_of(lax.div(kv, 2) * 128, 128), 128)
        prepare(
            kc_b[:, lanes], vc_b[:, lanes], kt_b[:, lanes], vt_b[:, lanes], scalars[1], second,
            keys_b, values_b, NODES,
        )
        prepare(
            kc_l[:, lanes], vc_l[:, lanes], kt_l[:, lanes], vt_l[:, lanes], scalars[3], second,
            keys_l, values_l, LIGHT,
        )

        def per_pair(step, inner):
            attend_head_pair(kv * 4 + step, head_base, refs, (scalars[0], scalars[2]))
            return inner

        return lax.fori_loop(0, 4, per_pair, carry)

    lax.fori_loop(0, 4, per_kv, 0)


def attention(scalars, sinks, *arrays):
    vmem = pl.BlockSpec(memory_space=pltpu.VMEM)
    smem = pl.BlockSpec(memory_space=pltpu.SMEM)
    return pl.pallas_call(
        attention_kernel,
        out_shape=(
            jax.ShapeDtypeStruct((NODES, HALF), BF16),
            jax.ShapeDtypeStruct((LIGHT, HALF), BF16),
        ),
        in_specs=[smem, smem] + [vmem] * len(arrays),
        out_specs=(vmem, vmem),
        scratch_shapes=[
            pltpu.VMEM((CACHE + NODES, 128), BF16),
            pltpu.VMEM((HD + SUMS, CACHE + NODES), BF16),
            pltpu.VMEM((CACHE + LIGHT, 128), BF16),
            pltpu.VMEM((HD + SUMS, CACHE + LIGHT), BF16),
            pltpu.VMEM((NODES, NODES), F32),
            pltpu.VMEM((LIGHT, LIGHT), F32),
        ],
        compiler_params=pltpu.CompilerParams(vmem_limit_bytes=60 * 1024 * 1024),
        cost_estimate=pl.CostEstimate(
            flops=32 * (512 * 1536 + 128 * 1152) * 256, bytes_accessed=8 * 2**20, transcendentals=0
        ),
        name="attend",
    )(scalars, sinks, *arrays)


def on_device(
    q_nodes, k_cache, v_cache, k_tree, v_tree, anc_bits, node_count, cache_len, sinks, o_weight
):
    core = lax.axis_index("core")
    swap = lambda x: lax.ppermute(x, "core", [(0, 1), (1, 0)])
    busy = lax.rem(lax.axis_index("gx") + core, 2) == 0

    def halves(x, width):
        first, second = x[..., :width], x[..., width:]
        return jnp.where(core == 0, first, second), jnp.where(core == 0, second, first)

    weight = jnp.pad(o_weight, ((0, 0), (0, 2 * COLS - D)))
    own_columns, other_columns = halves(weight, COLS)
    got_columns = swap(other_columns)
    chip_rows = jnp.where(
        core == 0,
        jnp.concatenate([own_columns, got_columns], axis=0),
        jnp.concatenate([got_columns, own_columns], axis=0),
    )
    gathered = lax.all_gather(chip_rows, ("gx", "gyc"), axis=0, tiled=True)

    own, sent = [], []
    for x, width in (
        (q_nodes[0], HALF), (k_cache[0], 256), (v_cache[0], 256), (k_tree[0], 256), (v_tree[0], 256)
    ):
        mine, other = halves(x, width)
        own.append(mine)
        sent.append(other)
    bits = anc_bits[0].T
    counts = jnp.stack([node_count[0], cache_len[0]])
    got = swap(tuple(sent) + (bits, counts))
    own = tuple(own) + (bits, counts)
    pick_b = [jnp.where(busy, a, b) for a, b in zip(own, got)]
    pick_l = [jnp.where(busy, b, a) for a, b in zip(own, got)]
    q_b, kc_b, vc_b, kt_b, vt_b, bits_b, counts_b = pick_b
    q_l, kc_l, vc_l, kt_l, vt_l, bits_l, counts_l = pick_l
    scalars = jnp.concatenate([counts_b, counts_l, (core * 32)[None].astype(jnp.int32)])
    att_b, att_l = attention(
        scalars, sinks, q_b, q_l[:LIGHT], kc_b, vc_b, kt_b, vt_b, kc_l, vc_l, kt_l[:LIGHT],
        vt_l[:LIGHT], bits_b, bits_l,
    )
    halves_own = jnp.concatenate([att_b, att_l], axis=0)
    halves_got = swap(halves_own)
    rows = jnp.where(
        core == 0,
        jnp.concatenate([halves_own, halves_got], axis=1),
        jnp.concatenate([halves_got, halves_own], axis=1),
    )
    out = jnp.dot(rows, gathered, preferred_element_type=F32).astype(BF16)
    out_got = swap(out)
    out = jnp.where(
        core == 0,
        jnp.concatenate([out, out_got], axis=1),
        jnp.concatenate([out_got, out], axis=1),
    )[:, :D]

    def place(x):
        light = jnp.pad(x[NODES:], ((0, NODES - LIGHT), (0, 0)))
        return jnp.where(busy, x[:NODES], light)[None]

    return place(rows), place(out)


def solution(mesh):
    split = Mesh(mesh.devices.reshape(8, 8, 2), ("gx", "gyc", "core"))
    every = ("gx", "gyc", "core")
    placed = tuple([P(every)] * 8) + (P(), P(every))
    return jax.shard_map(
        on_device, mesh=split, in_specs=placed, out_specs=(P(every), P(every)), check_vma=False
    )
```

time: 621 us -> 396 us (0.64)
  matrix products: 220 us -> 14.5 us
  waiting for transfers between devices: 103 us -> 215 us
  local copies, waits for them, and re-layouts: 94.1 us -> 4.77 us
  other arithmetic: 112 us -> 32.4 us
  Pallas kernels: 0 us -> 67.9 us
  loops' own time: 49.7 us -> 0 us
  starting transfers between devices: 21.9 us -> 45.9 us
    all_gather x1, waiting for transfers between devices: 0.01 us -> 208 us  [on_device(): gathered = lax.all_gather(chip_rows, ('gx', 'gyc'), axis=0, tiled=True)]
    dot_general x97 -> x1, matrix products: 220 us -> 14.5 us  [on_device(): out = jnp.dot(rows, gathered, preferred_element_type=F32).astype(BF16)]
    ppermute x16 -> x10, waiting for transfers between devices: 103 us -> 6.66 us  [on_device(): swap = lambda x: lax.ppermute(x, 'core', [(0, 1), (1, 0)])]
    reduce_sum x48 -> x0, other arithmetic: 85.7 us -> none  [the longest x24 78.5 us: per_kv_head(): jnp.sum(weight_cache, axis=1)]
    pallas_call x0 -> x1, Pallas kernels: none -> 67.9 us  [attention(): pl.pallas_call(attention_kernel, out_shape=(jax.ShapeDtypeStruct((NODES,...]
    another operation x6 -> x0, loops' own time: 49.7 us -> none  [the longest x3 49.4 us: attend_rows(): per_head = lax.map(per_kv_head, jnp.arange(KVH, dtype=jnp.int32))]
    dynamic_slice x76 -> x0, local copies, waits for them, and re-layouts: 36 us -> none  [the longest x24 15.3 us: attend_rows(): per_head = lax.map(per_kv_head, jnp.arange(KVH, dtype=jnp.int32))]
    select_n x0 -> x19, other arithmetic: none -> 28 us  [the longest x6 7.87 us: on_device(): pick_l = [jnp.where(busy, b, a) for a, b in zip(own, got)]]
  transfers between devices with their start and end apart: 17 -> 11, of which waited for: 4 -> 5; matrix products, arithmetic and copies ran while one was open for 65% -> 8% of each run, Pallas kernels for 0% -> 17%
where the time goes in v1:
time: 396 us
  waiting for transfers between devices  215 us (54%)
  Pallas kernels  67.9 us (17%)
  starting transfers between devices  45.9 us (12%)
  other arithmetic  32.4 us (8%)
  between operations  15.5 us (4%)
  matrix products  14.5 us (4%)
  local copies, waits for them, and re-layouts  4.77 us (1%)
    all_gather x1, waiting for transfers between devices, on_device(): gathered = lax.all_gather(chip_rows, ('gx', 'gyc'), axis=0, tiled=True)  208 us
    pallas_call x1, Pallas kernels, attention(): pl.pallas_call(attention_kernel, out_shape=(jax.ShapeDtypeStruct((NODES,...  67.9 us
    ppermute x10, starting transfers between devices, on_device(): swap = lambda x: lax.ppermute(x, 'core', [(0, 1), (1, 0)])  45.8 us
    dot_general x1, matrix products, on_device(): out = jnp.dot(rows, gathered, preferred_element_type=F32).astype(BF16)  14.5 us
  transfers between devices with their start and end apart: 11, of which 5 were waited for; matrix products, arithmetic and copies ran while one was open for 8% of the time, Pallas kernels for 17%

profile of v1, /device:TPU:1, one launch (start us, length us, event | category | flops | bytes accessed | tf_op | source)
XLA Modules:
  0.0 395.6 jit_solution(17019585930978671540)
XLA Ops:
  7.2 0.0 all-gather.2.cloned.1.call-start
  7.2 1.1 broadcast_select_fusion.18
  8.3 0.0 copy-start.5
  8.3 1.5 collective-permute-start.8
  9.8 0.9 collective-permute-done.8
  10.7 0.7 maximum_select_fusion.2
  11.4 0.0 all-gather.2.cloned.1.call-update
  11.5 0.0 copy-start.2
  11.5 0.0 copy-start.3
  11.5 3.9 broadcast_select_fusion
  15.4 0.4 collective-permute-start.1
  15.7 0.7 broadcast_select_fusion.11
  16.5 0.2 collective-permute-start.5
  16.6 0.7 broadcast_select_fusion.13
  17.4 0.4 collective-permute-start.4
  19.0 0.1 pad_add_fusion
  19.1 0.2 collective-permute-start
  19.3 0.8 broadcast_select_fusion.3
  20.1 0.4 collective-permute-start.3
  20.5 0.8 broadcast_select_fusion.5
  21.3 0.2 collective-permute-start.6
  21.5 0.1 broadcast_select_fusion.22
  21.6 0.6 pad_add_fusion.1.scalars
  22.2 0.3 collective-permute-done.6
  22.5 0.2 collective-permute-start.2
  22.7 0.6 broadcast_select_fusion.19
  23.4 0.8 broadcast_select_fusion.15
  24.1 2.2 broadcast_select_fusion.16
  26.3 0.6 slice_select_fusion.3.vt_l
  27.0 1.5 slice_select_fusion.4.kt_l
  28.4 2.1 broadcast_select_fusion.7
  30.6 1.1 broadcast_select_fusion.8
  31.7 3.4 broadcast_select_fusion.2
  35.1 1.9 slice_select_fusion.2.q_light
  37.0 67.9 %attend.1 = (bf16[512,2048]{1,0:T(8,128)(2,1)}, bf16[128,2048]{1,0:T(8,128)(2,1)}) custom-call(s32[5]{0:T(128)} %pad_add_fusion.1.scalars, f32[64]{0:T(128)} %sinks.1, bf16[512,2048]{1,0:T(8,128)(2,1)} %get-tuple-element.12.q_busy, bf16[128,2048]{1,0:T(8,128)(2,1)} %slice_select_fusion.2.q_light, bf16[1024,256]{1,0:T(8,128)(2,1)} %get-tuple-element.17.kc_b, ...), custom_call_target="tpu_custom_call" | custom-call | flops 7650410496 | bytes 8388608 | tf_op jit(solution)/shard_map/attend/pallas_call | solution.py:152
  104.9 1.9 constant_dynamic-update-slice_fusion.1
  106.8 0.3 collective-permute-start.7
  107.1 4.9 %collective-permute-done.7 = bf16[640,2048]{1,0:T(8,128)(2,1)S(1)} collective-permute-done((bf16[640,2048]{1,0:T(8,128)(2,1)S(1)}, bf16[640,2048]{1,0:T(8,128)(2,1)S(1)}, u32[]{:S(2)}, u32[]{:S(2)}) %collective-permute-start.7) | collective-permute-done | bytes 2621472 | tf_op jit(solution)/shard_map/ppermute | solution.py:180
  112.0 3.8 maximum_select_fusion
  115.8 208.1 %all-gather.2.cloned.1.call-done = bf16[4096,1536]{1,0:T(8,128)(2,1)} async-done(((bf16[64,1536]{1,0:T(8,128)(2,1)}), bf16[4096,1536]{1,0:T(8,128)(2,1)}) %all-gather.2.cloned.1.call-update) | async-done | bytes 12582928 | tf_op jit(solution)/shard_map/all_gather | solution.py:195
  323.8 14.5 %convolution_convert_fusion = bf16[640,1536]{1,0:T(8,128)(2,1)S(1)} fusion(bf16[640,4096]{1,0:T(8,128)(2,1)} %maximum_select_fusion, bf16[4096,1536]{1,0:T(8,128)(2,1)} %all-gather.2.cloned.1.call-done), kind=kOutput, calls=%fused_computation.4 | convolution fusion | flops 8054046720 | bytes 19791872 | tf_op jit(solution)/shard_map/dot_general | solution.py:224
  338.4 42.4 %collective-permute-start.9 = (bf16[640,1536]{1,0:T(8,128)(2,1)S(1)}, bf16[640,1536]{1,0:T(8,128)(2,1)S(1)}, u32[]{:S(2)}, u32[]{:S(2)}) collective-permute-start(bf16[640,1536]{1,0:T(8,128)(2,1)S(1)} %convolution_convert_fusion), channel_id=1, source_target_pairs={{0,1},{1,0},{2,3},{3,2},{4,5},{5,4},{6,7},{7,6},{8,9},{9,8},{10,11... | collective-permute-start | bytes 5898248 | tf_op jit(solution)/shard_map/ppermute | solution.py:180
  380.7 3.1 fusion
  383.8 0.5 collective-permute-done.9
  384.3 1.1 maximum_select_fusion.1
  385.4 0.1 slice.99
  385.4 0.6 fusion.1
  386.0 2.7 copy.12
  (22 shorter events, 0.1 us)
Async XLA Ops:
  7.2 8.6 %copy-start.4 = (bf16[1,512,512]{2,1,0:T(8,128)(2,1)S(1)}, bf16[1,512,512]{2,1,0:T(8,128)(2,1)}, u32[]{:S(2)}) copy-start(bf16[1,512,512]{2,1,0:T(8,128)(2,1)} %param.14) | copy-start | bytes 1572868
  7.2 316.7 %all-gather.2.cloned.1.call-start = ((), (), s32[]{:S(2)}) async-start(), calls=%async_computation | async-start | bytes 12779520 | tf_op jit(solution)/shard_map/all_gather | solution.py:195
  8.3 8.3 %copy-start.5 = (bf16[1,512,512]{2,1,0:T(8,128)(2,1)S(1)}, bf16[1,512,512]{2,1,0:T(8,128)(2,1)}, u32[]{:S(2)}) copy-start(bf16[1,512,512]{2,1,0:T(8,128)(2,1)} %param.13) | copy-start | bytes 1572868
  8.3 2.4 collective-permute-start.8
  11.5 7.8 %copy-start.2 = (bf16[1,1024,512]{2,1,0:T(8,128)(2,1)S(1)}, bf16[1,1024,512]{2,1,0:T(8,128)(2,1)}, u32[]{:S(2)}) copy-start(bf16[1,1024,512]{2,1,0:T(8,128)(2,1)} %param.12) | copy-start | bytes 3145732
  11.5 9.0 %copy-start.3 = (bf16[1,1024,512]{2,1,0:T(8,128)(2,1)S(1)}, bf16[1,1024,512]{2,1,0:T(8,128)(2,1)}, u32[]{:S(2)}) copy-start(bf16[1,1024,512]{2,1,0:T(8,128)(2,1)} %param.11) | copy-start | bytes 3145732
  15.4 5.9 %copy-start.7 = (s32[1,512,16]{1,2,0:T(8,128)S(1)}, s32[1,512,16]{1,2,0:T(8,128)}, u32[]{:S(2)}) copy-start(s32[1,512,16]{1,2,0:T(8,128)} %param.15) | copy-start | bytes 98308
  15.4 16.3 %collective-permute-start.1 = (bf16[512,2048]{1,0:T(8,128)(2,1)}, bf16[512,2048]{1,0:T(8,128)(2,1)}, u32[]{:S(2)}, u32[]{:S(2)}) collective-permute-start(bf16[512,2048]{1,0:T(8,128)(2,1)} %broadcast_select_fusion), channel_id=1, source_target_pairs={{0,1},{1,0},{2,3},{3,2},{4,5},{5,4},{6,7},{7,6},{8,9},{9,8},{10,11... | collective-permute-start | bytes 6291464 | tf_op jit(solution)/shard_map/ppermute | solution.py:180
  16.5 6.9 %collective-permute-start.5 = (bf16[512,256]{1,0:T(8,128)(2,1)}, bf16[512,256]{1,0:T(8,128)(2,1)S(1)}, u32[]{:S(2)}, u32[]{:S(2)}) collective-permute-start(bf16[512,256]{1,0:T(8,128)(2,1)} %broadcast_select_fusion.11), channel_id=1, source_target_pairs={{0,1},{1,0},{2,3},{3,2},{4,5},{5,4},{6,7},{7,6},{8,9},{9,8},{10,11... | collective-permute-start | bytes 786440 | tf_op jit(solution)/shard_map/ppermute | solution.py:180
  17.4 6.8 %collective-permute-start.4 = (bf16[512,256]{1,0:T(8,128)(2,1)}, bf16[512,256]{1,0:T(8,128)(2,1)}, u32[]{:S(2)}, u32[]{:S(2)}) collective-permute-start(bf16[512,256]{1,0:T(8,128)(2,1)} %broadcast_select_fusion.13), channel_id=1, source_target_pairs={{0,1},{1,0},{2,3},{3,2},{4,5},{5,4},{6,7},{7,6},{8,9},{9,8},{10,11... | collective-permute-start | bytes 786440 | tf_op jit(solution)/shard_map/ppermute | solution.py:180
  19.1 2.2 collective-permute-start
  20.1 8.3 %collective-permute-start.3 = (bf16[1024,256]{1,0:T(8,128)(2,1)}, bf16[1024,256]{1,0:T(8,128)(2,1)}, u32[]{:S(2)}, u32[]{:S(2)}) collective-permute-start(bf16[1024,256]{1,0:T(8,128)(2,1)} %broadcast_select_fusion.3), channel_id=1, source_target_pairs={{0,1},{1,0},{2,3},{3,2},{4,5},{5,4},{6,7},{7,6},{8,9},{9,8},{10,11... | collective-permute-start | bytes 1572872 | tf_op jit(solution)/shard_map/ppermute | solution.py:180
  21.3 1.2 collective-permute-start.6
  22.5 8.0 %collective-permute-start.2 = (bf16[1024,256]{1,0:T(8,128)(2,1)}, bf16[1024,256]{1,0:T(8,128)(2,1)S(1)}, u32[]{:S(2)}, u32[]{:S(2)}) collective-permute-start(bf16[1024,256]{1,0:T(8,128)(2,1)} %broadcast_select_fusion.5), channel_id=1, source_target_pairs={{0,1},{1,0},{2,3},{3,2},{4,5},{5,4},{6,7},{7,6},{8,9},{9,8},{10,11... | collective-permute-start | bytes 1572872 | tf_op jit(solution)/shard_map/ppermute | solution.py:180
  23.4 8.3 %copy-start.1 = (bf16[1,512,4096]{2,1,0:T(8,128)(2,1)S(1)}, bf16[1,512,4096]{2,1,0:T(8,128)(2,1)}, u32[]{:S(2)}) copy-start(bf16[1,512,4096]{2,1,0:T(8,128)(2,1)} %param.10) | copy-start | bytes 12582916
  104.9 1.9 copy-start.6
  106.8 5.2 %collective-permute-start.7 = (bf16[640,2048]{1,0:T(8,128)(2,1)S(1)}, bf16[640,2048]{1,0:T(8,128)(2,1)S(1)}, u32[]{:S(2)}, u32[]{:S(2)}) collective-permute-start(bf16[640,2048]{1,0:T(8,128)(2,1)S(1)} %constant_dynamic-update-slice_fusion), channel_id=1, source_target_pairs={{0,1},{1,0},{2,3},{3,2},{4,5},{5,4},{6,7},{7,6},{8,9},{9,8},{10,11... | collective-permute-start | bytes 7864328 | tf_op jit(solution)/shard_map/ppermute | solution.py:180
  115.8 265.0 %slice-start = ((bf16[640,4096]{1,0:T(8,128)(2,1)}), bf16[128,4096]{1,0:T(8,128)(2,1)S(1)}, s32[]{:S(2)}) async-start(bf16[640,4096]{1,0:T(8,128)(2,1)} %maximum_select_fusion), calls=%async_computation.1 | async-start | bytes 2097152 | tf_op jit(solution)/shard_map/slice | solution.py:233
  323.8 56.9 %copy-start = (bf16[640,4096]{1,0:T(8,128)(2,1)S(1)}, bf16[640,4096]{1,0:T(8,128)(2,1)}, u32[]{:S(2)}) copy-start(bf16[640,4096]{1,0:T(8,128)(2,1)} %maximum_select_fusion) | copy-start | bytes 15728644
  338.4 46.0 %collective-permute-start.9 = (bf16[640,1536]{1,0:T(8,128)(2,1)S(1)}, bf16[640,1536]{1,0:T(8,128)(2,1)S(1)}, u32[]{:S(2)}, u32[]{:S(2)}) collective-permute-start(bf16[640,1536]{1,0:T(8,128)(2,1)S(1)} %convolution_convert_fusion), channel_id=1, source_target_pairs={{0,1},{1,0},{2,3},{3,2},{4,5},{5,4},{6,7},{7,6},{8,9},{9,8},{10,11... | collective-permute-start | bytes 5898248 | tf_op jit(solution)/shard_map/ppermute | solution.py:180
Sparse Core Ops, SparseCore 0:
  11.6 312.2 all-gather.1

commit v2 on v1

--- a/solution.py
+++ b/solution.py
@@ -18,6 +18,8 @@
 SUMS = 16
 EXP_SCALE = 0.125 * 1.4426950408889634
 MASKED = -1.0e30
+PART = 512
+ROUND_AT = (1, 2, 4, 6, 11)
 F32 = jnp.float32
 BF16 = jnp.bfloat16
 
@@ -116,47 +118,143 @@
     out_l[:, lanes] = stacked.T.astype(BF16)
 
 
+class Ring:
+    def __init__(self, order, place, core):
+        self.order, self.place, self.core = order, place, core
+
+    def device(self, dim, by):
+        at = dict(self.place)
+        at[dim] = lax.rem(at[dim] + 4 + by, 4)
+        x, y, z = at["x"], at["y"], at["z"]
+        return (y * 2 + lax.div(z, 2), x * 2 + lax.rem(z, 2), self.core)
+
+    def slab(self, ref, phase, by, half):
+        dim = self.order[phase]
+        at = dict(self.place)
+        at[dim] = lax.rem(at[dim] + 4 + by, 4)
+        index = [at["y"], lax.div(at["z"], 2), at["x"], lax.rem(at["z"], 2), slice(None)]
+        full = self.order[:phase]
+        where = {"x": (2,), "y": (0,), "z": (1, 3)}
+        for name in full:
+            for axis in where[name]:
+                index[axis] = slice(None)
+        if half is not None:
+            axis = where[full[0]][0] if full else 4
+            size = {0: 4, 1: 2, 2: 4, 4: 64}[axis] // 2
+            index[axis] = pl.ds(half * size, size)
+        return ref.at[tuple(index)]
+
+
+def ring_copies(rings, chunks, gathered, send_sems, recv_sems, number):
+    phase, step = divmod(number, 2)
+    copies = []
+    for part, ring in enumerate(rings):
+        for side, by in enumerate((1, -1)):
+            if step == 0:
+                target = ring.slab(gathered[part], phase, 0, None)
+                source = chunks.at[part] if phase == 0 else target
+            else:
+                target = ring.slab(gathered[part], phase, -by, side)
+                source = target
+            copies.append(
+                pltpu.make_async_remote_copy(
+                    src_ref=source,
+                    dst_ref=target,
+                    send_sem=send_sems.at[number, part, side],
+                    recv_sem=recv_sems.at[number, part, side],
+                    device_id=ring.device(ring.order[phase], by),
+                    device_id_type=pl.DeviceIdType.MESH,
+                )
+            )
+    return copies
+
+
 def attention_kernel(
-    scalars, sinks, q_busy, q_light, kc_b, vc_b, kt_b, vt_b, kc_l, vc_l, kt_l, vt_l, bits_b, bits_l,
-    out_b, out_l, keys_b, values_b, keys_l, values_l, bias_b, bias_l,
+    scalars, sinks, chunks, q_busy, q_light, kc_b, vc_b, kt_b, vt_b, kc_l, vc_l, kt_l, vt_l,
+    bits_b, bits_l, out_b, out_l, gather_0, gather_1, gather_2, keys_b, values_b, keys_l, values_l,
+    bias_b, bias_l, send_sems, recv_sems, own_sems,
 ):
+    gx, gyc, core = lax.axis_index("gx"), lax.axis_index("gyc"), lax.axis_index("core")
+    place = {
+        "x": lax.div(gyc, 2), "y": lax.div(gx, 2), "z": lax.rem(gx, 2) * 2 + lax.rem(gyc, 2)
+    }
+    rings = [Ring(order, place, core) for order in ("xyz", "yzx", "zxy")]
+    gathered = (gather_0, gather_1, gather_2)
+
+    barrier = pltpu.get_barrier_semaphore()
+    for dim in "xyz":
+        for by in (1, -1):
+            pl.semaphore_signal(
+                barrier, inc=1, device_id=rings[0].device(dim, by),
+                device_id_type=pl.DeviceIdType.MESH,
+            )
+    pl.semaphore_wait(barrier, 6)
+
+    def ring_round(number):
+        return ring_copies(rings, chunks, gathered, send_sems, recv_sems, number)
+
+    own = [
+        pltpu.make_async_copy(
+            chunks.at[part], rings[part].slab(gathered[part], 0, 0, None), own_sems.at[part]
+        )
+        for part in range(3)
+    ]
+    for copy in ring_round(0) + own:
+        copy.start()
+
     build_bias(bits_b, bias_b, NODES, NODES)
     build_bias(bits_l, bias_l, LIGHT, LIGHT)
-    head_base = scalars[4]
+    head_base = core * 32
     refs = (q_busy, q_light, keys_b, values_b, keys_l, values_l, bias_b, bias_l, sinks, out_b, out_l)
 
-    def per_kv(kv, carry):
-        second = lax.rem(kv, 2) == 1
-        lanes = pl.ds(pl.multiple_of(lax.div(kv, 2) * 128, 128), 128)
-        prepare(
-            kc_b[:, lanes], vc_b[:, lanes], kt_b[:, lanes], vt_b[:, lanes], scalars[1], second,
-            keys_b, values_b, NODES,
-        )
-        prepare(
-            kc_l[:, lanes], vc_l[:, lanes], kt_l[:, lanes], vt_l[:, lanes], scalars[3], second,
-            keys_l, values_l, LIGHT,
-        )
-
-        def per_pair(step, inner):
-            attend_head_pair(kv * 4 + step, head_base, refs, (scalars[0], scalars[2]))
-            return inner
-
-        return lax.fori_loop(0, 4, per_pair, carry)
-
-    lax.fori_loop(0, 4, per_kv, 0)
-
-
-def attention(scalars, sinks, *arrays):
+    def per_pair(step, carry):
+        kv = lax.div(step, 4)
+
+        for number, when in enumerate(ROUND_AT):
+            @pl.when(step == when)
+            def _():
+                for copy in ring_round(number):
+                    copy.wait()
+                if number == 0:
+                    for copy in own:
+                        copy.wait()
+                for copy in ring_round(number + 1):
+                    copy.start()
+
+        @pl.when(lax.rem(step, 4) == 0)
+        def _():
+            second = lax.rem(kv, 2) == 1
+            lanes = pl.ds(pl.multiple_of(lax.div(kv, 2) * 128, 128), 128)
+            prepare(
+                kc_b[:, lanes], vc_b[:, lanes], kt_b[:, lanes], vt_b[:, lanes], scalars[1], second,
+                keys_b, values_b, NODES,
+            )
+            prepare(
+                kc_l[:, lanes], vc_l[:, lanes], kt_l[:, lanes], vt_l[:, lanes], scalars[3], second,
+                keys_l, values_l, LIGHT,
+            )
+
+        attend_head_pair(step, head_base, refs, (scalars[0], scalars[2]))
+        return carry
+
+    lax.fori_loop(0, 16, per_pair, 0)
+    for copy in ring_round(5):
+        copy.wait()
+
+
+def attention(scalars, sinks, chunks, *arrays):
     vmem = pl.BlockSpec(memory_space=pltpu.VMEM)
     smem = pl.BlockSpec(memory_space=pltpu.SMEM)
+    hbm = pl.BlockSpec(memory_space=pl.ANY)
     return pl.pallas_call(
         attention_kernel,
         out_shape=(
             jax.ShapeDtypeStruct((NODES, HALF), BF16),
             jax.ShapeDtypeStruct((LIGHT, HALF), BF16),
-        ),
-        in_specs=[smem, smem] + [vmem] * len(arrays),
-        out_specs=(vmem, vmem),
+        )
+        + (jax.ShapeDtypeStruct((4, 2, 4, 2, 64, PART), BF16),) * 3,
+        in_specs=[smem, smem] + [vmem] * (len(arrays) + 1),
+        out_specs=(vmem, vmem, hbm, hbm, hbm),
         scratch_shapes=[
             pltpu.VMEM((CACHE + NODES, 128), BF16),
             pltpu.VMEM((HD + SUMS, CACHE + NODES), BF16),
@@ -164,13 +262,18 @@
             pltpu.VMEM((HD + SUMS, CACHE + LIGHT), BF16),
             pltpu.VMEM((NODES, NODES), F32),
             pltpu.VMEM((LIGHT, LIGHT), F32),
+            pltpu.SemaphoreType.DMA((6, 3, 2)),
+            pltpu.SemaphoreType.DMA((6, 3, 2)),
+            pltpu.SemaphoreType.DMA((3,)),
         ],
-        compiler_params=pltpu.CompilerParams(vmem_limit_bytes=60 * 1024 * 1024),
+        compiler_params=pltpu.CompilerParams(
+            vmem_limit_bytes=60 * 1024 * 1024, collective_id=0, has_side_effects=True
+        ),
         cost_estimate=pl.CostEstimate(
             flops=32 * (512 * 1536 + 128 * 1152) * 256, bytes_accessed=8 * 2**20, transcendentals=0
         ),
         name="attend",
-    )(scalars, sinks, *arrays)
+    )(scalars, sinks, chunks, *arrays)
 
 
 def on_device(
@@ -192,7 +295,7 @@
         jnp.concatenate([own_columns, got_columns], axis=0),
         jnp.concatenate([got_columns, own_columns], axis=0),
     )
-    gathered = lax.all_gather(chip_rows, ("gx", "gyc"), axis=0, tiled=True)
+    chunks = jnp.transpose(chip_rows.reshape(64, 3, PART), (1, 0, 2))
 
     own, sent = [], []
     for x, width in (
@@ -209,9 +312,9 @@
     pick_l = [jnp.where(busy, b, a) for a, b in zip(own, got)]
     q_b, kc_b, vc_b, kt_b, vt_b, bits_b, counts_b = pick_b
     q_l, kc_l, vc_l, kt_l, vt_l, bits_l, counts_l = pick_l
-    scalars = jnp.concatenate([counts_b, counts_l, (core * 32)[None].astype(jnp.int32)])
-    att_b, att_l = attention(
-        scalars, sinks, q_b, q_l[:LIGHT], kc_b, vc_b, kt_b, vt_b, kc_l, vc_l, kt_l[:LIGHT],
+    scalars = jnp.concatenate([counts_b, counts_l])
+    att_b, att_l, *gathered = attention(
+        scalars, sinks, chunks, q_b, q_l[:LIGHT], kc_b, vc_b, kt_b, vt_b, kc_l, vc_l, kt_l[:LIGHT],
         vt_l[:LIGHT], bits_b, bits_l,
     )
     halves_own = jnp.concatenate([att_b, att_l], axis=0)
@@ -221,7 +324,13 @@
         jnp.concatenate([halves_own, halves_got], axis=1),
         jnp.concatenate([halves_got, halves_own], axis=1),
     )
-    out = jnp.dot(rows, gathered, preferred_element_type=F32).astype(BF16)
+    out = jnp.concatenate(
+        [
+            jnp.dot(rows, part.reshape(4096, PART), preferred_element_type=F32).astype(BF16)
+            for part in gathered
+        ],
+        axis=1,
+    )
     out_got = swap(out)
     out = jnp.where(
         core == 0,

time: 396 us -> 152 us (0.38)
  waiting for transfers between devices: 215 us -> 4.96 us
  starting transfers between devices: 45.9 us -> 6.12 us
  other arithmetic: 32.4 us -> 46 us
  between operations: 15.5 us -> 2.26 us
  Pallas kernels: 67.9 us -> 79.9 us
  matrix products: 14.5 us -> 10.3 us
    all_gather x1 -> x0, waiting for transfers between devices: 208 us -> none  [on_device(): gathered = lax.all_gather(chip_rows, ('gx', 'gyc'), axis=0, tiled=True)]
    ppermute x10, starting transfers between devices: 45.8 us -> 6.12 us  [on_device(): swap = lambda x: lax.ppermute(x, 'core', [(0, 1), (1, 0)])]
    select_n x1, other arithmetic: 1.07 us -> 22 us  [on_device(): jnp.where(core == 0, jnp.concatenate([out, out_got], axis=1), jnp.concate...]
    pallas_call x1, Pallas kernels: 67.9 us -> 79.9 us  [attention(): pl.pallas_call(attention_kernel, out_shape=(jax.ShapeDtypeStruct((NODES,...]
    dot_general x1 -> x3, matrix products: 14.5 us -> 10.3 us  [on_device(): jnp.dot(rows, part.reshape(4096, PART), preferred_element_type=F32)]
  transfers between devices with their start and end apart: 11 -> 10, of which waited for: 5 -> 2; matrix products, arithmetic and copies ran while one was open for 8% -> 11% of each run, Pallas kernels for 17% -> 0%
where the time goes in v2:
time: 152 us
  Pallas kernels  79.9 us (53%)
  other arithmetic  46 us (30%)
  matrix products  10.3 us (7%)
  starting transfers between devices  6.12 us (4%)
  waiting for transfers between devices  4.96 us (3%)
  between operations  2.26 us (1%)
  local copies, waits for them, and re-layouts  2.12 us (1%)
    pallas_call x1, Pallas kernels, attention(): pl.pallas_call(attention_kernel, out_shape=(jax.ShapeDtypeStruct((NODES,...  79.9 us
    select_n x1, other arithmetic, on_device(): jnp.where(core == 0, jnp.concatenate([out, out_got], axis=1), jnp.concate...  22 us
    dot_general x3, matrix products, on_device(): jnp.dot(rows, part.reshape(4096, PART), preferred_element_type=F32)  10.3 us
    ppermute x10, starting transfers between devices, on_device(): swap = lambda x: lax.ppermute(x, 'core', [(0, 1), (1, 0)])  6.12 us
    select_n x5, other arithmetic, halves(): jnp.where(core == 0, second, first)  5.94 us
    broadcast_in_dim x2, other arithmetic, place(): return jnp.where(busy, x[:NODES], light)[None]  5.25 us
    ppermute x10, waiting for transfers between devices, on_device(): swap = lambda x: lax.ppermute(x, 'core', [(0, 1), (1, 0)])  4.96 us
    select_n x6, other arithmetic, on_device(): pick_l = [jnp.where(busy, b, a) for a, b in zip(own, got)]  4.93 us
  transfers between devices with their start and end apart: 10, of which 2 were waited for; matrix products, arithmetic and copies ran while one was open for 11% of the time, Pallas kernels for 0%

profile of v2, /device:TPU:1, one launch (start us, length us, event | category | flops | bytes accessed | tf_op | source)
XLA Modules:
  0.0 151.7 jit_solution(4956279518853722087)
XLA Ops:
  2.0 0.1 pad_add_fusion
  2.1 1.4 collective-permute-start
  3.5 0.1 collective-permute-start.7
  3.6 1.0 broadcast_select_fusion.18
  4.6 0.5 collective-permute-start.1
  5.1 1.1 broadcast_select_fusion.11
  6.2 0.2 collective-permute-start.6
  6.3 1.1 broadcast_select_fusion.13
  7.4 0.5 collective-permute-start.5
  7.9 1.3 broadcast_select_fusion.5
  9.2 0.0 copy-start.6
  9.2 0.0 copy-start.3
  9.2 0.1 broadcast_select_fusion.3
  9.3 0.0 copy-start.4
  9.3 2.5 %broadcast_select_fusion = bf16[512,2048]{1,0:T(8,128)(2,1)S(1)} fusion(pred[]{:T(512)S(6)} %eq.5, bf16[512,4096]{1,0:T(8,128)(2,1)} %bitcast.33), kind=kLoop, calls=%fused_computation.6 | loop fusion | flops 1048576 | bytes 6291457 | tf_op jit(solution)/shard_map/jit(_where)/select_n | solution.py:288
  11.8 0.0 copy-start.2
  11.8 0.2 collective-permute-start.2
  12.0 0.1 broadcast_select_fusion.22
  12.1 0.7 pad_add_fusion.1.scalars
  12.7 0.4 collective-permute-start.4
  13.2 0.6 broadcast_select_fusion.19
  13.8 0.1 collective-permute-start.3
  13.9 0.7 fusion.2.chunks
  14.6 0.8 broadcast_select_fusion.16
  15.4 0.8 broadcast_select_fusion.15
  16.1 0.6 slice_select_fusion.4.kt_l
  16.8 0.6 slice_select_fusion.3.vt_l
  17.4 0.0 collective-permute-done.4
  17.4 1.1 broadcast_select_fusion.7
  18.5 1.1 broadcast_select_fusion.8
  19.6 0.0 collective-permute-done.2
  19.6 1.7 %broadcast_select_fusion.2 = (bf16[512,2048]{1,0:T(8,128)(2,1)}, bf16[512,2048]{1,0:T(8,128)(2,1)S(1)}) fusion(bf16[512,2048]{1,0:T(8,128)(2,1)S(1)} %collective-permute-done.2, pred[]{:T(512)S(6)} %eq.4, bf16[512,4096]{1,0:T(8,128)(2,1)S(1)} %bitcast.34, pred[]{:T(512)S(6)} %eq.5), kind=kLoop, calls=%fused_computation.8 | loop fusion | flops 2097152 | bytes 10485762 | tf_op jit(solution)/shard_map/jit(_where)/select_n | solution.py:311
  21.3 0.8 slice_select_fusion.2.q_light
  22.1 79.9 %attend.1 = (bf16[512,2048]{1,0:T(8,128)(2,1)}, bf16[128,2048]{1,0:T(8,128)(2,1)}, bf16[4,2,4,2,64,512]{5,4,3,2,1,0:T(8,128)(2,1)}, bf16[4,2,4,2,64,512]{5,4,3,2...) custom-call(s32[4]{0:T(128)} %pad_add_fusion.1.scalars, f32[64]{0:T(128)} %sinks.1, bf16[3,64,512]{2,1,0:T(8,128)(2,1)} %fusion.2.chunks, ...), custom_call_target="tpu_custom_call" | custom-call | flops 7650410496 | bytes 8388608 | tf_op jit(solution)/shard_map/attend/pallas_call | solution.py:249
  102.0 1.9 %constant_dynamic-update-slice_fusion.1 = bf16[640,2048]{1,0:T(8,128)(2,1)S(1)} fusion(bf16[512,2048]{1,0:T(8,128)(2,1)} %get-tuple-element.7), kind=kLoop, calls=%fused_computation.40 | loop fusion | bytes 4194304
  104.0 2.1 %collective-permute-start.8 = (bf16[640,2048]{1,0:T(8,128)(2,1)S(1)}, bf16[640,2048]{1,0:T(8,128)(2,1)S(1)}, u32[]{:S(2)}, u32[]{:S(2)}) collective-permute-start(bf16[640,2048]{1,0:T(8,128)(2,1)S(1)} %constant_dynamic-update-slice_fusion), channel_id=1, source_target_pairs={{0,1},{1,0},{2,3},{3,2},{4,5},{5,4},{6,7},{7,6},{8,9},{9,8},{10,11... | collective-permute-start | bytes 7864328 | tf_op jit(solution)/shard_map/ppermute | solution.py:283
  106.1 4.5 %collective-permute-done.8 = bf16[640,2048]{1,0:T(8,128)(2,1)S(1)} collective-permute-done((bf16[640,2048]{1,0:T(8,128)(2,1)S(1)}, bf16[640,2048]{1,0:T(8,128)(2,1)S(1)}, u32[]{:S(2)}, u32[]{:S(2)}) %collective-permute-start.8) | collective-permute-done | bytes 2621472 | tf_op jit(solution)/shard_map/ppermute | solution.py:283
  110.6 2.0 %maximum_select_fusion = bf16[640,4096]{1,0:T(8,128)(2,1)S(1)} fusion(bf16[640,2048]{1,0:T(8,128)(2,1)S(1)} %collective-permute-done.8, bf16[640,2048]{1,0:T(8,128)(2,1)S(1)} %constant_dynamic-update-slice_fusion, pred[]{:T(512)S(6)} %eq.5), kind=kLoop, calls=%fused_computation | loop fusion | flops 23592960 | bytes 10485761 | tf_op jit(solution)/shard_map/jit(_where)/select_n | solution.py:322
  112.6 3.4 %convolution_convert_fusion = bf16[640,512]{0,1:T(8,128)(2,1)S(1)} fusion(bf16[640,4096]{1,0:T(8,128)(2,1)S(1)} %maximum_select_fusion, bf16[4096,512]{1,0:T(8,128)(2,1)S(1)} %bitcast.50), kind=kOutput, calls=%fused_computation.10 | convolution fusion | flops 2684682240 | bytes 10092544 | tf_op jit(solution)/shard_map/dot_general | solution.py:329
  116.1 3.4 %convolution_convert_fusion.1 = bf16[640,512]{0,1:T(8,128)(2,1)S(1)} fusion(bf16[640,4096]{1,0:T(8,128)(2,1)S(1)} %maximum_select_fusion, bf16[4096,512]{1,0:T(8,128)(2,1)S(1)} %bitcast.49), kind=kOutput, calls=%fused_computation.11 | convolution fusion | flops 2684682240 | bytes 10092544 | tf_op jit(solution)/shard_map/dot_general | solution.py:329
  119.6 3.4 %convolution_convert_fusion.2 = bf16[640,512]{0,1:T(8,128)(2,1)S(1)} fusion(bf16[640,4096]{1,0:T(8,128)(2,1)S(1)} %maximum_select_fusion, bf16[4096,512]{1,0:T(8,128)(2,1)S(1)} %bitcast.48), kind=kOutput, calls=%fused_computation.12 | convolution fusion | flops 2684682240 | bytes 10092544 | tf_op jit(solution)/shard_map/dot_general | solution.py:329
  123.0 0.2 pad_maximum_fusion
  123.2 0.7 collective-permute-start.9
  123.9 0.1 slice.97
  124.0 3.1 %fusion = bf16[1,512,4096]{2,1,0:T(8,128)(2,1)} fusion(bf16[640,4096]{1,0:T(8,128)(2,1)S(1)} %maximum_select_fusion, bf16[128,4096]{1,0:T(8,128)(2,1)S(1)} %slice.97, pred[]{:T(512)S(6)} %eq.4), kind=kLoop, calls=%fused_computation.2 | loop fusion | flops 2097152 | bytes 9437185 | tf_op jit(solution)/shard_map/broadcast_in_dim | solution.py:343
  127.1 0.4 collective-permute-done.9
  127.5 22.0 %maximum_select_fusion.1 = bf16[640,3072]{0,1:T(8,128)(2,1)S(1)} fusion(bf16[640,1536]{0,1:T(8,128)(2,1)S(1)} %collective-permute-done.9, bf16[640,512]{0,1:T(8,128)(2,1)S(1)} %convolution_convert_fusion, bf16[640,512]{0,1:T(8,128)(2,1)S(1)} %convolution_convert_fusion.1, bf16[640,512]{0,1:T(8,128)(2,1)S(1)} %convolution_convert_fusion.2, pred[]{:T(512)S(6)} %eq.5), kind=kLoop, calls=%fused_computation.3 | loop fusion | flops 33423360 | bytes 7864321 | tf_op jit(solution)/shard_map/jit(_where)/select_n | solution.py:335
  149.6 2.1 %fusion.1 = bf16[1,512,2880]{1,2,0:T(8,128)(2,1)} fusion(bf16[640,3072]{0,1:T(8,128)(2,1)S(1)} %maximum_select_fusion.1, bf16[128,2880]{0,1:T(8,128)(2,1)S(1)} %slice.99, pred[]{:T(512)S(6)} %eq.4), kind=kLoop, calls=%fused_computation.5 | loop fusion | flops 1474560 | bytes 6635521 | tf_op jit(solution)/shard_map/broadcast_in_dim | solution.py:343
  (26 shorter events, 0.1 us)
Async XLA Ops:
  0.6 8.5 %copy-start.1 = (bf16[1,1024,512]{2,1,0:T(8,128)(2,1)S(1)}, bf16[1,1024,512]{2,1,0:T(8,128)(2,1)}, u32[]{:S(2)}) copy-start(bf16[1,1024,512]{2,1,0:T(8,128)(2,1)} %param.12) | copy-start | bytes 3145732
  2.1 9.7 %collective-permute-start = (s32[2]{0:T(128)S(1)}, s32[2]{0:T(128)S(1)}, u32[]{:S(2)}, u32[]{:S(2)}) collective-permute-start(s32[2]{0:T(128)S(1)} %pad_add_fusion), channel_id=1, source_target_pairs={{0,1},{1,0},{2,3},{3,2},{4,5},{5,4},{6,7},{7,6},{8,9},{9,8},{10,11... | collective-permute-start | bytes 32 | tf_op jit(solution)/shard_map/ppermute | solution.py:283
  3.5 9.2 %collective-permute-start.7 = (s32[16,512]{1,0:T(8,128)}, s32[16,512]{1,0:T(8,128)S(1)}, u32[]{:S(2)}, u32[]{:S(2)}) collective-permute-start(s32[16,512]{1,0:T(8,128)} %bitcast.47), channel_id=1, source_target_pairs={{0,1},{1,0},{2,3},{3,2},{4,5},{5,4},{6,7},{7,6},{8,9},{9,8},{10,11... | collective-permute-start | bytes 98312 | tf_op jit(solution)/shard_map/ppermute | solution.py:283
  4.6 9.2 %collective-permute-start.1 = (bf16[32,1536]{1,0:T(8,128)(2,1)S(1)}, bf16[32,1536]{1,0:T(8,128)(2,1)S(1)}, u32[]{:S(2)}, u32[]{:S(2)}) collective-permute-start(bf16[32,1536]{1,0:T(8,128)(2,1)S(1)} %get-tuple-element.23), channel_id=1, source_target_pairs={{0,1},{1,0},{2,3},{3,2},{4,5},{5,4},{6,7},{7,6},{8,9},{9,8},{10,11... | collective-permute-start | bytes 294920 | tf_op jit(solution)/shard_map/ppermute | solution.py:283
  6.2 9.2 %collective-permute-start.6 = (bf16[512,256]{1,0:T(8,128)(2,1)S(1)}, bf16[512,256]{1,0:T(8,128)(2,1)S(1)}, u32[]{:S(2)}, u32[]{:S(2)}) collective-permute-start(bf16[512,256]{1,0:T(8,128)(2,1)S(1)} %broadcast_select_fusion.11), channel_id=1, source_target_pairs={{0,1},{1,0},{2,3},{3,2},{4,5},{5,4},{6,7},{7,6},{8,9},{9,8},{10,11... | collective-permute-start | bytes 786440 | tf_op jit(solution)/shard_map/ppermute | solution.py:283
  7.4 7.2 %collective-permute-start.5 = (bf16[512,256]{1,0:T(8,128)(2,1)S(1)}, bf16[512,256]{1,0:T(8,128)(2,1)S(1)}, u32[]{:S(2)}, u32[]{:S(2)}) collective-permute-start(bf16[512,256]{1,0:T(8,128)(2,1)S(1)} %broadcast_select_fusion.13), channel_id=1, source_target_pairs={{0,1},{1,0},{2,3},{3,2},{4,5},{5,4},{6,7},{7,6},{8,9},{9,8},{10,11... | collective-permute-start | bytes 786440 | tf_op jit(solution)/shard_map/ppermute | solution.py:283
  9.2 4.0 %copy-start.6 = (s32[1,512,16]{1,2,0:T(8,128)S(1)}, s32[1,512,16]{1,2,0:T(8,128)}, u32[]{:S(2)}) copy-start(s32[1,512,16]{1,2,0:T(8,128)} %param.15) | copy-start | bytes 98308
  9.2 5.4 %copy-start.3 = (bf16[1,512,512]{2,1,0:T(8,128)(2,1)S(1)}, bf16[1,512,512]{2,1,0:T(8,128)(2,1)}, u32[]{:S(2)}) copy-start(bf16[1,512,512]{2,1,0:T(8,128)(2,1)} %param.13) | copy-start | bytes 1572868
  9.3 6.1 %copy-start.4 = (bf16[1,512,512]{2,1,0:T(8,128)(2,1)S(1)}, bf16[1,512,512]{2,1,0:T(8,128)(2,1)}, u32[]{:S(2)}) copy-start(bf16[1,512,512]{2,1,0:T(8,128)(2,1)} %param.14) | copy-start | bytes 1572868
  11.8 6.7 %copy-start.2 = (bf16[1,1024,512]{2,1,0:T(8,128)(2,1)S(1)}, bf16[1,1024,512]{2,1,0:T(8,128)(2,1)}, u32[]{:S(2)}) copy-start(bf16[1,1024,512]{2,1,0:T(8,128)(2,1)} %param.11) | copy-start | bytes 3145732
  11.8 7.8 %collective-permute-start.2 = (bf16[512,2048]{1,0:T(8,128)(2,1)S(1)}, bf16[512,2048]{1,0:T(8,128)(2,1)S(1)}, u32[]{:S(2)}, u32[]{:S(2)}) collective-permute-start(bf16[512,2048]{1,0:T(8,128)(2,1)S(1)} %broadcast_select_fusion), channel_id=1, source_target_pairs={{0,1},{1,0},{2,3},{3,2},{4,5},{5,4},{6,7},{7,6},{8,9},{9,8},{10,11... | collective-permute-start | bytes 6291464 | tf_op jit(solution)/shard_map/ppermute | solution.py:283
  12.7 4.7 %collective-permute-start.4 = (bf16[1024,256]{1,0:T(8,128)(2,1)S(1)}, bf16[1024,256]{1,0:T(8,128)(2,1)S(1)}, u32[]{:S(2)}, u32[]{:S(2)}) collective-permute-start(bf16[1024,256]{1,0:T(8,128)(2,1)S(1)} %broadcast_select_fusion.3), channel_id=1, source_target_pairs={{0,1},{1,0},{2,3},{3,2},{4,5},{5,4},{6,7},{7,6},{8,9},{9,8},{10,11... | collective-permute-start | bytes 1572872 | tf_op jit(solution)/shard_map/ppermute | solution.py:283
  13.8 4.7 %collective-permute-start.3 = (bf16[1024,256]{1,0:T(8,128)(2,1)S(1)}, bf16[1024,256]{1,0:T(8,128)(2,1)S(1)}, u32[]{:S(2)}, u32[]{:S(2)}) collective-permute-start(bf16[1024,256]{1,0:T(8,128)(2,1)S(1)} %broadcast_select_fusion.5), channel_id=1, source_target_pairs={{0,1},{1,0},{2,3},{3,2},{4,5},{5,4},{6,7},{7,6},{8,9},{9,8},{10,11... | collective-permute-start | bytes 1572872 | tf_op jit(solution)/shard_map/ppermute | solution.py:283
  14.6 5.0 %copy-start = (bf16[1,512,4096]{2,1,0:T(8,128)(2,1)S(1)}, bf16[1,512,4096]{2,1,0:T(8,128)(2,1)}, u32[]{:S(2)}) copy-start(bf16[1,512,4096]{2,1,0:T(8,128)(2,1)} %param.10) | copy-start | bytes 12582916
  102.0 1.9 %copy-start.5 = (bf16[128,2048]{1,0:T(8,128)(2,1)S(1)}, bf16[128,2048]{1,0:T(8,128)(2,1)}, u32[]{:S(2)}) copy-start(bf16[128,2048]{1,0:T(8,128)(2,1)} %get-tuple-element.8) | copy-start | bytes 1572868
  104.0 8.7 %copy-start.9 = (bf16[4,2,4,2,64,512]{5,4,3,2,1,0:T(8,128)(2,1)S(1)}, bf16[4,2,4,2,64,512]{5,4,3,2,1,0:T(8,128)(2,1)}, u32[]{:S(2)}) copy-start(bf16[4,2,4,2,64,512]{5,4,3,2,1,0:T(8,128)(2,1)} %get-tuple-element.11) | copy-start | bytes 12582916
  104.0 6.6 %collective-permute-start.8 = (bf16[640,2048]{1,0:T(8,128)(2,1)S(1)}, bf16[640,2048]{1,0:T(8,128)(2,1)S(1)}, u32[]{:S(2)}, u32[]{:S(2)}) collective-permute-start(bf16[640,2048]{1,0:T(8,128)(2,1)S(1)} %constant_dynamic-update-slice_fusion), channel_id=1, source_target_pairs={{0,1},{1,0},{2,3},{3,2},{4,5},{5,4},{6,7},{7,6},{8,9},{9,8},{10,11... | collective-permute-start | bytes 7864328 | tf_op jit(solution)/shard_map/ppermute | solution.py:283
  112.6 3.5 %copy-start.8 = (bf16[4,2,4,2,64,512]{5,4,3,2,1,0:T(8,128)(2,1)S(1)}, bf16[4,2,4,2,64,512]{5,4,3,2,1,0:T(8,128)(2,1)}, u32[]{:S(2)}) copy-start(bf16[4,2,4,2,64,512]{5,4,3,2,1,0:T(8,128)(2,1)} %get-tuple-element.10) | copy-start | bytes 12582916
  116.1 3.5 %copy-start.7 = (bf16[4,2,4,2,64,512]{5,4,3,2,1,0:T(8,128)(2,1)S(1)}, bf16[4,2,4,2,64,512]{5,4,3,2,1,0:T(8,128)(2,1)}, u32[]{:S(2)}) copy-start(bf16[4,2,4,2,64,512]{5,4,3,2,1,0:T(8,128)(2,1)} %get-tuple-element.9) | copy-start | bytes 12582916
  123.2 4.3 %collective-permute-start.9 = (bf16[640,1536]{0,1:T(8,128)(2,1)S(1)}, bf16[640,1536]{0,1:T(8,128)(2,1)S(1)}, u32[]{:S(2)}, u32[]{:S(2)}) collective-permute-start(bf16[640,1536]{0,1:T(8,128)(2,1)S(1)} %pad_maximum_fusion), channel_id=1, source_target_pairs={{0,1},{1,0},{2,3},{3,2},{4,5},{5,4},{6,7},{7,6},{8,9},{9,8},{10,11... | collective-permute-start | bytes 5898248 | tf_op jit(solution)/shard_map/ppermute | solution.py:283

commit v3 on v1

v3 whole, which is shorter than its diff:
```python
import functools

import jax
import jax.numpy as jnp
from jax import lax
from jax.experimental import pallas as pl
from jax.experimental.pallas import tpu as pltpu
from jax.sharding import Mesh, PartitionSpec as P

HD = 64
NODES = 512
LIGHT = 128
CACHE = 1024
HALF = 2048
COLS = 1536
D = 2880
TILE = 256
SUMS = 16
EXP_SCALE = 0.125 * 1.4426950408889634
MASKED = -1.0e30
PART = 512
MESH = pl.DeviceIdType.MESH
WHERE = {"x": (2,), "y": (0,), "z": (1, 3)}
SIZES = (4, 2, 4, 2)
PLAN = (
    (1, ("own",), ("far",)),
    (2, ("far",), ("line", "face0")),
    (4, ("line",), ("line2", "face-", "face+")),
    (5, ("face0",), ("back0",)),
    (6, ("line2",), ("face2",)),
    (9, ("face-", "face+"), ("back-", "back+")),
    (11, ("face2",), ("back2",)),
)
NAMES = (
    "own", "far", "line", "line2", "face0", "face-", "face+", "face2", "back0", "back-", "back+",
    "back2",
)
LINES = {"0": 0, "-": -1, "+": 1, "2": 2}
F32 = jnp.float32
BF16 = jnp.bfloat16


def lane_ids(shape):
    return lax.broadcasted_iota(jnp.int32, shape, len(shape) - 1)


def row_ids(shape):
    return lax.broadcasted_iota(jnp.int32, shape, len(shape) - 2)


def build_bias(bits_ref, bias_ref, keys, nodes):
    shift = row_ids((32, nodes))
    for word in range(keys // 32):
        row = jnp.broadcast_to(bits_ref[word : word + 1, :nodes], (32, nodes))
        bit = jnp.bitwise_and(lax.shift_right_logical(row, shift), 1)
        bias_ref[word * 32 : word * 32 + 32, :] = jnp.where(bit > 0, 0.0, MASKED)


def spread_keys(pair, second):
    wide = pair.astype(F32)
    turned = pltpu.roll(wide, HD, 1)
    take_own = (lane_ids(wide.shape) < HD) == jnp.logical_not(second)
    return jnp.where(take_own, wide, turned)


def turn_values(pair, second):
    turned = pair.astype(F32).T
    return jnp.where(second, turned[HD:], turned[:HD])


def prepare(k_cache, v_cache, k_tree, v_tree, length, second, keys_ref, values_ref, tree):
    keys = spread_keys(k_cache, second)
    keys_ref[pl.ds(0, CACHE), :] = jnp.where(row_ids(keys.shape) < length[:, :128], keys, 0.0).astype(BF16)
    keys_ref[pl.ds(CACHE, tree), :] = spread_keys(k_tree, second).astype(BF16)
    values = turn_values(v_cache, second)
    live = lane_ids(values.shape) < length
    values_ref[pl.ds(0, HD), pl.ds(0, CACHE)] = jnp.where(live, values, 0.0).astype(BF16)
    live = lane_ids((SUMS, CACHE)) < length
    values_ref[pl.ds(HD, SUMS), pl.ds(0, CACHE)] = jnp.where(live, 1.0, 0.0).astype(BF16)
    values_ref[pl.ds(0, HD), pl.ds(CACHE, tree)] = turn_values(v_tree, second).astype(BF16)
    values_ref[pl.ds(HD, SUMS), pl.ds(CACHE, tree)] = jnp.ones((SUMS, tree), BF16)


def contract_last(a, b):
    return lax.dot_general(a, b, (((1,), (1,)), ((), ())), preferred_element_type=F32)


def attend_tile(keys_ref, values_ref, queries, bias, sink, tree, node_ok):
    cache_scores = contract_last(keys_ref[pl.ds(0, CACHE), :], queries)
    tree_scores = contract_last(keys_ref[pl.ds(CACHE, tree), :], queries) + bias
    row_max = jnp.maximum(
        jnp.max(cache_scores, axis=0, keepdims=True), jnp.max(tree_scores, axis=0, keepdims=True)
    )
    row_max = jnp.maximum(row_max, sink)
    cache_weights = jnp.exp2((cache_scores - row_max) * EXP_SCALE).astype(BF16)
    tree_weights = jnp.exp2((tree_scores - row_max) * EXP_SCALE).astype(BF16)
    sums = jnp.dot(values_ref[:, pl.ds(0, CACHE)], cache_weights, preferred_element_type=F32)
    sums += jnp.dot(values_ref[:, pl.ds(CACHE, tree)], tree_weights, preferred_element_type=F32)
    denominator = sums[HD : HD + 1] + jnp.exp2((sink - row_max) * EXP_SCALE)
    return sums[:HD] * jnp.where(node_ok, 1.0 / denominator, 0.0)


def attend_head_pair(pair, core, refs, counts):
    (q_busy, q_light, keys_b, values_b, keys_l, values_l, bias_b, bias_l, sinks, att) = refs
    count_b, count_l = counts
    lanes = pl.ds(pl.multiple_of(pair * 128, 128), 128)
    out_lanes = pl.ds(pl.multiple_of(core * HALF + pair * 128, 128), 128)
    first_head = core * 32
    sink_even = sinks[first_head + 2 * pair] * 8.0
    sink_odd = sinks[first_head + 2 * pair + 1] * 8.0
    for tile in range(NODES // TILE):
        rows = pl.ds(tile * TILE, TILE)
        tree = (tile + 1) * TILE
        queries = q_busy[rows, lanes]
        left = lane_ids(queries.shape) < HD
        bias = bias_b[pl.ds(0, tree), rows]
        node_ok = lane_ids((1, TILE)) + tile * TILE < count_b
        zero = jnp.zeros_like(queries)
        even = attend_tile(
            keys_b, values_b, jnp.where(left, queries, zero), bias, sink_even, tree, node_ok
        )
        odd = attend_tile(
            keys_b, values_b, jnp.where(left, zero, queries), bias, sink_odd, tree, node_ok
        )
        att[rows, out_lanes] = jnp.concatenate([even, odd], axis=0).T.astype(BF16)
    queries = q_light[:, lanes]
    left = lane_ids(queries.shape) < HD
    zero = jnp.zeros_like(queries)
    both = jnp.concatenate([jnp.where(left, queries, zero), jnp.where(left, zero, queries)], axis=0)
    columns = lane_ids((1, TILE))
    sink = jnp.where(columns < LIGHT, sink_even, sink_odd)
    node_ok = jnp.where(columns < LIGHT, columns, columns - LIGHT) < count_l
    bias = jnp.concatenate([bias_l[...], bias_l[...]], axis=1)
    result = attend_tile(keys_l, values_l, both, bias, sink, LIGHT, node_ok)
    stacked = jnp.concatenate([result[:, :LIGHT], result[:, LIGHT:]], axis=0)
    att[pl.ds(NODES, LIGHT), out_lanes] = stacked.T.astype(BF16)


class Ring:
    def __init__(self, order, place, core, weights):
        self.order, self.place, self.core, self.weights = order, place, core, weights

    def moved(self, dim, by):
        return lax.rem(self.place[dim] + 4 + by, 4)

    def device(self, dim, by):
        at = dict(self.place)
        at[dim] = self.moved(dim, by)
        x, y, z = at["x"], at["y"], at["z"]
        return (y * 2 + lax.div(z, 2), x * 2 + lax.rem(z, 2), self.core)

    def block(self, offsets, whole=False, half=None):
        at = {dim: self.moved(dim, by) for dim, by in zip(self.order, offsets)}
        index = [at["y"], lax.div(at["z"], 2), at["x"], lax.rem(at["z"], 2), slice(None)]
        axes = WHERE[self.order[0]] if whole else (4,)
        if whole:
            for axis in axes:
                index[axis] = slice(None)
        if half is not None:
            size = (SIZES[axes[0]] if whole else 64) // 2
            index[axes[0]] = pl.ds(half * size, size)
        return self.weights.at[tuple(index)]

    def send(self, name, side):
        by = (1, -1)[side]
        if name == "own":
            return 0, self.block((0, 0, 0))
        if name == "far":
            return 0, self.block((-by, 0, 0), half=side)
        if name == "line":
            return 1, self.block((0, 0, 0), whole=True)
        if name == "line2":
            return 1, self.block((0, -by, 0), whole=True, half=side)
        line = LINES[name[-1]]
        if name.startswith("face"):
            return 2, self.block((0, line, 0), whole=True)
        return 2, self.block((0, line, -by), whole=True, half=side)


def message(rings, name, send_sems, recv_sems):
    number = NAMES.index(name)
    copies = []
    for part, ring in enumerate(rings):
        for side in range(2):
            axis, block = ring.send(name, side)
            copies.append(
                pltpu.make_async_remote_copy(
                    src_ref=block, dst_ref=block,
                    send_sem=send_sems.at[number, part, side],
                    recv_sem=recv_sems.at[number, part, side],
                    device_id=ring.device(ring.order[axis], (1, -1)[side]),
                    device_id_type=MESH,
                )
            )
    return copies


def whole_kernel(
    sinks, q_hbm, kc_hbm, vc_hbm, kt_hbm, vt_hbm, meta_hbm, w_hbm, att_hbm, proj_hbm,
    q_b, kc_b, vc_b, kt_b, vt_b, meta_b, q_l, kc_l, vc_l, kt_l, vt_l, meta_l,
    weights_0, weights_1, weights_2, att, proj, keys_b, values_b, keys_l, values_l, bias_b, bias_l,
    send_sems, recv_sems, load_sems, load_send, load_recv, w_sems, att_send, att_recv, att_sem,
    proj_send, proj_recv, proj_sem,
):
    gx, gyc, core = lax.axis_index("gx"), lax.axis_index("gyc"), lax.axis_index("core")
    partner = (gx, gyc, 1 - core)
    busy = lax.rem(gx + core, 2) == 0
    place = {
        "x": lax.div(gyc, 2), "y": lax.div(gx, 2), "z": lax.rem(gx, 2) * 2 + lax.rem(gyc, 2)
    }
    weights = (weights_0, weights_1, weights_2)
    rings = [Ring(order, place, core, w) for order, w in zip(("xyz", "yzx", "zxy"), weights)]

    def by_role(run):
        pl.when(busy)(lambda: run(True))
        pl.when(jnp.logical_not(busy))(lambda: run(False))

    def to_partner(source, target, send, recv):
        return pltpu.make_async_remote_copy(
            src_ref=source, dst_ref=target, send_sem=send, recv_sem=recv, device_id=partner,
            device_id_type=MESH,
        )

    def load_pairs(heavy, piece, half):
        rows, q, kc, vc, kt, vt, meta = (
            (NODES, q_b, kc_b, vc_b, kt_b, vt_b, meta_b)
            if heavy
            else (LIGHT, q_l, kc_l, vc_l, kt_l, vt_l, meta_l)
        )
        if piece[0] == "q":
            return [
                (
                    q_hbm.at[pl.ds(0, rows), pl.ds(half * HALF + piece[1] * 512, 512)],
                    q.at[:, pl.ds(pl.multiple_of(piece[1] * 512, 512), 512)],
                )
            ]
        if piece[0] == "meta":
            return [(meta_hbm, meta)]
        source = pl.ds(half * 256 + piece[1] * 128, 128)
        target = pl.ds(pl.multiple_of(piece[1] * 128, 128), 128)
        return [
            (kc_hbm.at[:, source], kc.at[:, target]),
            (vc_hbm.at[:, source], vc.at[:, target]),
            (kt_hbm.at[pl.ds(0, rows), source], kt.at[:, target]),
            (vt_hbm.at[pl.ds(0, rows), source], vt.at[:, target]),
        ]

    def slot(piece):
        return {"meta": 0, "q": 1, "kv": 5}[piece[0]] + piece[1] * (4 if piece[0] == "kv" else 1)

    def local_loads(heavy, piece):
        pairs = load_pairs(heavy, piece, core)
        return [
            pltpu.make_async_copy(a, b, load_sems.at[slot(piece) + i])
            for i, (a, b) in enumerate(pairs)
        ]

    def remote_loads(heavy, piece):
        pairs = load_pairs(heavy, piece, 1 - core)
        return [
            to_partner(a, b, load_send.at[slot(piece) + i], load_recv.at[slot(piece) + i])
            for i, (a, b) in enumerate(pairs)
        ]

    def start_loads(heavy):
        pieces = [("meta", 0), ("kv", 0)] + [("q", kv) for kv in range(4)]
        pieces.insert(5, ("kv", 1))
        for piece in pieces:
            for copy in remote_loads(heavy, piece) + local_loads(heavy, piece):
                copy.start()

    def wait_loads(piece):
        def run(heavy):
            for copy in local_loads(heavy, piece):
                copy.wait()
            for copy in remote_loads(not heavy, piece):
                copy.wait_recv()

        by_role(run)

    def wait_sends():
        def run(heavy):
            for piece in [("meta", 0)] + [("q", kv) for kv in range(4)] + [("kv", 0), ("kv", 1)]:
                for copy in remote_loads(heavy, piece):
                    copy.wait_send()

        by_role(run)

    barrier = pltpu.get_barrier_semaphore()
    for dim in "xyz":
        for by in (1, -1):
            pl.semaphore_signal(
                barrier, inc=1, device_id=rings[0].device(dim, by), device_id_type=MESH
            )
    pl.semaphore_signal(barrier, inc=1, device_id=partner, device_id_type=MESH)
    pl.semaphore_wait(barrier, 7)

    rows = pl.ds(pl.multiple_of(core * 32, 32), 32)
    chunk_local, chunk_remote = [], []
    for part, ring in enumerate(rings):
        target = ring.block((0, 0, 0)).at[rows]
        chunk_local.append(
            pltpu.make_async_copy(w_hbm.at[core, part], target, w_sems.at[0, part])
        )
        chunk_remote.append(
            to_partner(w_hbm.at[1 - core, part], target, w_sems.at[1, part], w_sems.at[2, part])
        )
    for copy in chunk_remote + chunk_local:
        copy.start()
    by_role(start_loads)
    for local, remote, part in zip(chunk_local, chunk_remote, range(3)):
        local.wait()
        remote.wait_send()
        other = pl.ds(pl.multiple_of(32 - core * 32, 32), 32)
        landed = rings[part].block((0, 0, 0)).at[other]
        to_partner(landed, landed, w_sems.at[1, part], w_sems.at[2, part]).wait_recv()

    def start(name):
        for copy in message(rings, name, send_sems, recv_sems):
            copy.start()

    def finish(name):
        for copy in message(rings, name, send_sems, recv_sems):
            copy.wait()

    start("own")
    wait_loads(("meta", 0))
    build_bias(meta_b, bias_b, NODES, NODES)
    build_bias(meta_l, bias_l, LIGHT, LIGHT)
    count_b, count_l = meta_b[16:17, :TILE], meta_l[16:17, :TILE]
    refs = (q_b, q_l, keys_b, values_b, keys_l, values_l, bias_b, bias_l, sinks, att)

    def att_half(side, kv):
        return att.at[:, pl.ds(pl.multiple_of(side * HALF + kv * 512, 512), 512)]

    def att_swap(kv):
        own = att_half(core, kv)
        return to_partner(own, own, att_send.at[kv], att_recv.at[kv])

    def per_pair(step, carry):
        kv = lax.div(step, 4)
        for when, waits, starts in PLAN:

            @pl.when(step == when)
            def _():
                for name in waits:
                    finish(name)
                for name in starts:
                    start(name)

        @pl.when(lax.rem(step, 4) == 0)
        def _():
            pair = lax.div(kv, 2)
            second = lax.rem(kv, 2) == 1
            wait_loads(("q", kv))
            pl.when(jnp.logical_not(second))(lambda: wait_loads(("kv", pair)))
            lanes = pl.ds(pl.multiple_of(pair * 128, 128), 128)
            prepare(
                kc_b[:, lanes], vc_b[:, lanes], kt_b[:, lanes], vt_b[:, lanes], meta_b[17:18, :],
                second, keys_b, values_b, NODES,
            )
            prepare(
                kc_l[:, lanes], vc_l[:, lanes], kt_l[:, lanes], vt_l[:, lanes], meta_l[17:18, :],
                second, keys_l, values_l, LIGHT,
            )

        attend_head_pair(step, core, refs, (count_b, count_l))

        @pl.when((lax.rem(step, 4) == 0) & (step > 0))
        def _():
            att_swap(kv - 1).start()

        return carry

    lax.fori_loop(0, 16, per_pair, 0)
    for name in ("back0", "back-", "back+"):
        finish(name)
    wait_sends()
    att_swap(3).start()
    finish("back2")
    for kv in range(4):
        att_swap(kv).wait_send()
        other = att_half(1 - core, kv)
        to_partner(other, other, att_send.at[kv], att_recv.at[kv]).wait_recv()

    def att_store(heavy):
        first, count = (0, NODES) if heavy else (NODES, LIGHT)
        return pltpu.make_async_copy(
            att.at[pl.ds(first, count)], att_hbm.at[pl.ds(0, count)], att_sem
        )

    by_role(lambda heavy: att_store(heavy).start())

    def proj_block(heavy, part):
        first, count = (0, NODES) if heavy else (NODES, LIGHT)
        return proj.at[part, pl.ds(first, count)]

    def proj_place(heavy, side, part):
        count = NODES if heavy else LIGHT
        columns = pl.ds(pl.multiple_of(side * COLS + part * PART, PART), PART)
        return proj_hbm.at[pl.ds(0, count), columns]

    def proj_copies(heavy, part):
        own = pltpu.make_async_copy(
            proj_block(heavy, part), proj_place(heavy, core, part), proj_sem.at[part]
        )
        sent = to_partner(
            proj_block(not heavy, part), proj_place(not heavy, core, part), proj_send.at[part],
            proj_recv.at[part],
        )
        return own, sent

    def start_proj(heavy, part):
        own, sent = proj_copies(heavy, part)
        sent.start()
        own.start()

    def finish_proj(heavy, part):
        own, sent = proj_copies(heavy, part)
        own.wait()
        sent.wait_send()
        landed = proj_place(heavy, 1 - core, part)
        to_partner(landed, landed, proj_send.at[part], proj_recv.at[part]).wait_recv()

    for part in range(3):

        def per_block(block, carry, part=part):
            rows = pl.ds(pl.multiple_of(block * 320, 64), 320)
            total = None
            for gx_at in range(8):
                term = jnp.dot(
                    att[rows, gx_at * 512 : gx_at * 512 + 512],
                    weights[part][gx_at // 2, gx_at % 2].reshape(512, PART),
                    preferred_element_type=F32,
                )
                total = term if total is None else total + term
            proj[part, rows, :] = total.astype(BF16)
            return carry

        lax.fori_loop(0, 2, per_block, 0)
        if part > 0:
            by_role(functools.partial(start_proj, part=part - 1))
    by_role(lambda heavy: att_store(heavy).wait())
    by_role(functools.partial(start_proj, part=2))
    for part in range(3):
        by_role(functools.partial(finish_proj, part=part))


def whole(sinks, *arrays):
    smem = pl.BlockSpec(memory_space=pltpu.SMEM)
    hbm = pl.BlockSpec(memory_space=pl.ANY)
    dma = pltpu.SemaphoreType.DMA

    def role(rows):
        return [
            pltpu.VMEM((rows, HALF), BF16),
            pltpu.VMEM((CACHE, 256), BF16),
            pltpu.VMEM((CACHE, 256), BF16),
            pltpu.VMEM((rows, 256), BF16),
            pltpu.VMEM((rows, 256), BF16),
            pltpu.VMEM((24, CACHE), jnp.int32),
        ]

    return pl.pallas_call(
        whole_kernel,
        out_shape=(
            jax.ShapeDtypeStruct((NODES, 2 * HALF), BF16),
            jax.ShapeDtypeStruct((NODES, 2 * COLS), BF16),
        ),
        in_specs=[smem] + [hbm] * len(arrays),
        out_specs=(hbm, hbm),
        scratch_shapes=role(NODES)
        + role(LIGHT)
        + [pltpu.VMEM((4, 2, 4, 2, 64, PART), BF16)] * 3
        + [
            pltpu.VMEM((NODES + LIGHT, 2 * HALF), BF16),
            pltpu.VMEM((3, NODES + LIGHT, PART), BF16),
            pltpu.VMEM((CACHE + NODES, 128), BF16),
            pltpu.VMEM((HD + SUMS, CACHE + NODES), BF16),
            pltpu.VMEM((CACHE + LIGHT, 128), BF16),
            pltpu.VMEM((HD + SUMS, CACHE + LIGHT), BF16),
            pltpu.VMEM((NODES, NODES), F32),
            pltpu.VMEM((LIGHT, LIGHT), F32),
            dma((len(NAMES), 3, 2)), dma((len(NAMES), 3, 2)),
            dma((13,)), dma((13,)), dma((13,)), dma((3, 3)),
            dma((4,)), dma((4,)), dma, dma((3,)), dma((3,)), dma((3,)),
        ],
        compiler_params=pltpu.CompilerParams(
            vmem_limit_bytes=60 * 1024 * 1024, collective_id=0, has_side_effects=True
        ),
        cost_estimate=pl.CostEstimate(
            flops=32 * (512 * 1536 + 128 * 1152) * 256, bytes_accessed=8 * 2**20, transcendentals=0
        ),
        name="whole",
    )(sinks, *arrays)


def on_device(
    q_nodes, k_cache, v_cache, k_tree, v_tree, anc_bits, node_count, cache_len, sinks, o_weight
):
    busy = lax.rem(lax.axis_index("gx") + lax.axis_index("core"), 2) == 0
    weight = jnp.pad(o_weight, ((0, 0), (0, 2 * COLS - D)))
    weight = jnp.transpose(weight.reshape(32, 2, 3, PART), (1, 2, 0, 3))
    bits = jnp.pad(anc_bits[0].T, ((0, 0), (0, CACHE - NODES)))
    ones = jnp.ones((1, CACHE), jnp.int32)
    meta = jnp.concatenate(
        [bits, ones * node_count[0], ones * cache_len[0], jnp.zeros((6, CACHE), jnp.int32)], axis=0
    )
    attended, projected = whole(
        sinks, q_nodes[0], k_cache[0], v_cache[0], k_tree[0], v_tree[0], meta, weight
    )
    kept = (jnp.arange(NODES) < jnp.where(busy, NODES, LIGHT))[:, None]

    def place(x):
        return jnp.where(kept, x, jnp.zeros_like(x))[None]

    return place(attended), place(projected[:, :D])


def solution(mesh):
    split = Mesh(mesh.devices.reshape(8, 8, 2), ("gx", "gyc", "core"))
    every = ("gx", "gyc", "core")
    placed = tuple([P(every)] * 8) + (P(), P(every))
    return jax.shard_map(
        on_device, mesh=split, in_specs=placed, out_specs=(P(every), P(every)), check_vma=False
    )
```

time: 396 us -> 109 us (0.28)
  waiting for transfers between devices: 215 us -> 0 us
  starting transfers between devices: 45.9 us -> 0 us
  Pallas kernels: 67.9 us -> 93.2 us
  other arithmetic: 32.4 us -> 8.23 us
  matrix products: 14.5 us -> 0 us
  between operations: 15.5 us -> 1.98 us
    all_gather x1 -> x0, waiting for transfers between devices: 208 us -> none  [on_device(): gathered = lax.all_gather(chip_rows, ('gx', 'gyc'), axis=0, tiled=True)]
    ppermute x10 -> x0, starting transfers between devices: 45.8 us -> none  [on_device(): swap = lambda x: lax.ppermute(x, 'core', [(0, 1), (1, 0)])]
    select_n x19 -> x0, other arithmetic: 28 us -> none  [the longest x6 7.87 us: on_device(): pick_l = [jnp.where(busy, b, a) for a, b in zip(own, got)]]
    pallas_call x1, Pallas kernels: 67.9 us -> 93.2 us  [whole(): pl.pallas_call(whole_kernel, out_shape=(jax.ShapeDtypeStruct((NODES, 2 *...]
    dot_general x1 -> x0, matrix products: 14.5 us -> none  [on_device(): out = jnp.dot(rows, gathered, preferred_element_type=F32).astype(BF16)]
    ppermute x10 -> x0, waiting for transfers between devices: 6.66 us -> none  [on_device(): swap = lambda x: lax.ppermute(x, 'core', [(0, 1), (1, 0)])]
  transfers between devices with their start and end apart: 11 -> 0, of which waited for: 5 -> 0; matrix products, arithmetic and copies ran while one was open for 8% -> 0% of each run, Pallas kernels for 17% -> 0%
where the time goes in v3:
time: 109 us; the launch traced here: 108 us
  Pallas kernels  93.2 us (86%)
  other arithmetic  8.23 us (8%)
  local copies, waits for them, and re-layouts  4.94 us (5%)
  between operations  1.98 us (2%)
    pallas_call x1, Pallas kernels, whole(): pl.pallas_call(whole_kernel, out_shape=(jax.ShapeDtypeStruct((NODES, 2 *...  93.2 us
    broadcast_in_dim x2, other arithmetic, place(): return jnp.where(kept, x, jnp.zeros_like(x))[None]  6.75 us
    unnamed x1, local copies, waits for them, and re-layouts  2.74 us

profile of v3, /device:TPU:1, one launch (start us, length us, event | category | flops | bytes accessed | tf_op | source)
XLA Modules:
  0.0 108.3 jit_solution(1443064220891551300)
XLA Ops:
  0.7 0.9 pad.9
  1.6 0.3 reshape.11
  1.9 0.8 copy.16
  3.3 0.1 pad.11.clone
  4.0 0.1 pad.12.clone
  4.1 0.1 pad.13.clone
  4.2 1.5 %fusion.1.meta_hbm = s32[24,1024]{1,0:T(8,128)} fusion(s32[16,512]{1,0:T(8,128)} %bitcast.18, s32[24]{0:T(128)S(1)} %pad.13.clone, s32[24]{0:T(128)S(1)} %pad.12.clone, s32[24]{0:T(128)S(1)} %pad.11.clone), kind=kLoop, calls=%fused_computation.5 | loop fusion | flops 73728 | bytes 131360 | tf_op jit(solution)/shard_map/concatenate | solution.py:506
  5.7 93.2 %whole.1 = (bf16[512,4096]{1,0:T(8,128)(2,1)}, bf16[512,3072]{1,0:T(8,128)(2,1)}) custom-call(f32[64]{0:T(128)} %sinks.1, bf16[512,4096]{1,0:T(8,128)(2,1)} %bitcast.19, bf16[1024,512]{1,0:T(8,128)(2,1)} %bitcast.20, bf16[1024,512]{1,0:T(8,128)(2,1)} %bitcast.21, bf16[512,512]{1,0:T(8,128)(2,1)} %bitcast.22, bf16[512,512]{1,0:T(8,128)(2,1)} %bitcast.23, ...), custom_call_target="tpu_custom_call" | custom-call | flops 7650410496 | bytes 8388608 | tf_op jit(solution)/shard_map/whole/pallas_call | solution.py:464
  98.9 2.2 %select_bitcast_fusion.1 = bf16[1,512,2880]{2,1,0:T(8,128)(2,1)S(1)} fusion(bf16[512,3072]{1,0:T(8,128)(2,1)} %get-tuple-element.5, pred[512]{0:T(512)(128)(4,1)S(1)} %iota_compare_fusion), kind=kLoop, calls=%fused_computation.1 | loop fusion | flops 1474560 | bytes 5898752 | tf_op jit(solution)/shard_map/broadcast_in_dim | solution.py:515
  101.1 2.7 %copy.14 = bf16[1,512,2880]{1,2,0:T(8,128)(2,1)} copy(bf16[1,512,2880]{2,1,0:T(8,128)(2,1)S(1)} %select_bitcast_fusion.1) | data formatting | bytes 5898240
  103.8 4.5 %select_bitcast_fusion = bf16[1,512,4096]{2,1,0:T(8,128)(2,1)} fusion(bf16[512,4096]{1,0:T(8,128)(2,1)} %get-tuple-element.4, pred[512]{0:T(512)(128)(4,1)S(1)} %iota_compare_fusion), kind=kLoop, calls=%fused_computation | loop fusion | flops 2097152 | bytes 8389120 | tf_op jit(solution)/shard_map/broadcast_in_dim | solution.py:515
  (2 shorter events, 0.0 us)

commit v4 on v3

--- a/solution.py
+++ b/solution.py
@@ -12,28 +12,28 @@
 LIGHT = 128
 CACHE = 1024
 HALF = 2048
-COLS = 1536
 D = 2880
 TILE = 256
 SUMS = 16
 EXP_SCALE = 0.125 * 1.4426950408889634
 MASKED = -1.0e30
 PART = 512
+PART_COLS = 480
 MESH = pl.DeviceIdType.MESH
 WHERE = {"x": (2,), "y": (0,), "z": (1, 3)}
 SIZES = (4, 2, 4, 2)
 PLAN = (
-    (1, ("own",), ("far",)),
-    (2, ("far",), ("line", "face0")),
-    (4, ("line",), ("line2", "face-", "face+")),
-    (5, ("face0",), ("back0",)),
-    (6, ("line2",), ("face2",)),
-    (9, ("face-", "face+"), ("back-", "back+")),
-    (11, ("face2",), ("back2",)),
+    (1, ("own",), ("far", "l-", "l+", "f-", "f+")),
+    (3, ("far",), ("l2", "f2")),
+    (5, ("l0", "l-", "l+", "l2"), ("line2", "face-", "face+")),
+    (6, ("f0", "f-", "f+", "f2"), ("back0",)),
+    (7, ("line2",), ("face2",)),
+    (11, ("face-", "face+"), ("back-", "back+")),
+    (14, ("face2",), ("back2",)),
 )
 NAMES = (
-    "own", "far", "line", "line2", "face0", "face-", "face+", "face2", "back0", "back-", "back+",
-    "back2",
+    "own", "far", "l0", "l-", "l+", "l2", "line2", "f0", "f-", "f+", "f2", "face-", "face+",
+    "face2", "back0", "back-", "back+", "back2",
 )
 LINES = {"0": 0, "-": -1, "+": 1, "2": 2}
 F32 = jnp.float32
@@ -85,53 +85,101 @@
     return lax.dot_general(a, b, (((1,), (1,)), ((), ())), preferred_element_type=F32)
 
 
-def attend_tile(keys_ref, values_ref, queries, bias, sink, tree, node_ok):
-    cache_scores = contract_last(keys_ref[pl.ds(0, CACHE), :], queries)
-    tree_scores = contract_last(keys_ref[pl.ds(CACHE, tree), :], queries) + bias
-    row_max = jnp.maximum(
-        jnp.max(cache_scores, axis=0, keepdims=True), jnp.max(tree_scores, axis=0, keepdims=True)
-    )
-    row_max = jnp.maximum(row_max, sink)
-    cache_weights = jnp.exp2((cache_scores - row_max) * EXP_SCALE).astype(BF16)
-    tree_weights = jnp.exp2((tree_scores - row_max) * EXP_SCALE).astype(BF16)
-    sums = jnp.dot(values_ref[:, pl.ds(0, CACHE)], cache_weights, preferred_element_type=F32)
-    sums += jnp.dot(values_ref[:, pl.ds(CACHE, tree)], tree_weights, preferred_element_type=F32)
-    denominator = sums[HD : HD + 1] + jnp.exp2((sink - row_max) * EXP_SCALE)
-    return sums[:HD] * jnp.where(node_ok, 1.0 / denominator, 0.0)
+def fold_max(scores):
+    rows = scores.shape[0]
+    return jnp.max(scores.reshape(rows // 8, 8, TILE), axis=0)
+
+
+class Unit:
+    def __init__(self, keys, values, queries, bias, tree, sink, node_ok, scores):
+        self.keys, self.values, self.queries, self.bias = keys, values, queries, bias
+        self.sink, self.node_ok, self.scores = sink, node_ok, scores
+        self.chunks = [(at, TILE) for at in range(0, CACHE, TILE)]
+        self.chunks += [(CACHE + at, min(TILE, tree)) for at in range(0, tree, TILE)]
+        self.peak = None
+        self.total = None
+
+    def score(self, number):
+        at, count = self.chunks[number]
+        scores = contract_last(self.keys[pl.ds(at, count), :], self.queries)
+        if at >= CACHE:
+            scores = scores + self.bias(at - CACHE, count)
+        self.scores[pl.ds(at, count), :] = scores
+        peak = fold_max(scores)
+        self.peak = peak if self.peak is None else jnp.maximum(self.peak, peak)
+
+    def settle(self):
+        self.row_max = jnp.maximum(jnp.max(self.peak, axis=0, keepdims=True), self.sink)
+
+    def weigh(self, number):
+        at, count = self.chunks[number]
+        weights = jnp.exp2((self.scores[pl.ds(at, count), :] - self.row_max) * EXP_SCALE)
+        term = jnp.dot(
+            self.values[:, pl.ds(at, count)], weights.astype(BF16), preferred_element_type=F32
+        )
+        self.total = term if self.total is None else self.total + term
+
+    def result(self):
+        denominator = self.total[HD : HD + 1] + jnp.exp2((self.sink - self.row_max) * EXP_SCALE)
+        return self.total[:HD] * jnp.where(self.node_ok, 1.0 / denominator, 0.0)
 
 
 def attend_head_pair(pair, core, refs, counts):
-    (q_busy, q_light, keys_b, values_b, keys_l, values_l, bias_b, bias_l, sinks, att) = refs
+    (q_busy, q_light, keys_b, values_b, keys_l, values_l, bias_b, bias_l, sinks, att, scores) = refs
     count_b, count_l = counts
     lanes = pl.ds(pl.multiple_of(pair * 128, 128), 128)
     out_lanes = pl.ds(pl.multiple_of(core * HALF + pair * 128, 128), 128)
     first_head = core * 32
     sink_even = sinks[first_head + 2 * pair] * 8.0
     sink_odd = sinks[first_head + 2 * pair + 1] * 8.0
+    columns = lane_ids((1, TILE))
+    units = []
     for tile in range(NODES // TILE):
         rows = pl.ds(tile * TILE, TILE)
-        tree = (tile + 1) * TILE
-        queries = q_busy[rows, lanes]
-        left = lane_ids(queries.shape) < HD
-        bias = bias_b[pl.ds(0, tree), rows]
-        node_ok = lane_ids((1, TILE)) + tile * TILE < count_b
-        zero = jnp.zeros_like(queries)
-        even = attend_tile(
-            keys_b, values_b, jnp.where(left, queries, zero), bias, sink_even, tree, node_ok
-        )
-        odd = attend_tile(
-            keys_b, values_b, jnp.where(left, zero, queries), bias, sink_odd, tree, node_ok
-        )
-        att[rows, out_lanes] = jnp.concatenate([even, odd], axis=0).T.astype(BF16)
-    queries = q_light[:, lanes]
-    left = lane_ids(queries.shape) < HD
-    zero = jnp.zeros_like(queries)
-    both = jnp.concatenate([jnp.where(left, queries, zero), jnp.where(left, zero, queries)], axis=0)
-    columns = lane_ids((1, TILE))
-    sink = jnp.where(columns < LIGHT, sink_even, sink_odd)
-    node_ok = jnp.where(columns < LIGHT, columns, columns - LIGHT) < count_l
-    bias = jnp.concatenate([bias_l[...], bias_l[...]], axis=1)
-    result = attend_tile(keys_l, values_l, both, bias, sink, LIGHT, node_ok)
+        for odd, sink in enumerate((sink_even, sink_odd)):
+
+            def queries(rows=rows, odd=odd):
+                both = q_busy[rows, lanes]
+                return jnp.where((lane_ids(both.shape) < HD) == (odd == 0), both, jnp.zeros_like(both))
+
+            units.append(
+                Unit(
+                    keys_b, values_b, queries(),
+                    lambda at, count, rows=rows: bias_b[pl.ds(at, count), rows],
+                    (tile + 1) * TILE, sink, columns + tile * TILE < count_b,
+                    scores.at[len(units) % 2],
+                )
+            )
+    both = q_light[:, lanes]
+    left = lane_ids(both.shape) < HD
+    zero = jnp.zeros_like(both)
+    both = jnp.concatenate([jnp.where(left, both, zero), jnp.where(left, zero, both)], axis=0)
+    units.append(
+        Unit(
+            keys_l, values_l, both,
+            lambda at, count: jnp.concatenate([bias_l[...], bias_l[...]], axis=1), LIGHT,
+            jnp.where(columns < LIGHT, sink_even, sink_odd),
+            jnp.where(columns < LIGHT, columns, columns - LIGHT) < count_l,
+            scores.at[len(units) % 2],
+        )
+    )
+    results = []
+    for number in range(len(units) + 1):
+        ahead = units[number] if number < len(units) else None
+        behind = units[number - 1] if number > 0 else None
+        for chunk in range(6):
+            if ahead is not None and chunk < len(ahead.chunks):
+                ahead.score(chunk)
+            if behind is not None and chunk < len(behind.chunks):
+                behind.weigh(chunk)
+        if behind is not None:
+            results.append(behind.result())
+        if ahead is not None:
+            ahead.settle()
+        if number in (2, 4):
+            rows = pl.ds((number // 2 - 1) * TILE, TILE)
+            att[rows, out_lanes] = jnp.concatenate(results[-2:], axis=0).T.astype(BF16)
+    result = results[-1]
     stacked = jnp.concatenate([result[:, :LIGHT], result[:, LIGHT:]], axis=0)
     att[pl.ds(NODES, LIGHT), out_lanes] = stacked.T.astype(BF16)
 
@@ -167,11 +215,11 @@
             return 0, self.block((0, 0, 0))
         if name == "far":
             return 0, self.block((-by, 0, 0), half=side)
-        if name == "line":
-            return 1, self.block((0, 0, 0), whole=True)
         if name == "line2":
             return 1, self.block((0, -by, 0), whole=True, half=side)
         line = LINES[name[-1]]
+        if len(name) == 2:
+            return {"l": 1, "f": 2}[name[0]], self.block((line, 0, 0))
         if name.startswith("face"):
             return 2, self.block((0, line, 0), whole=True)
         return 2, self.block((0, line, -by), whole=True, half=side)
@@ -198,7 +246,7 @@
 def whole_kernel(
     sinks, q_hbm, kc_hbm, vc_hbm, kt_hbm, vt_hbm, meta_hbm, w_hbm, att_hbm, proj_hbm,
     q_b, kc_b, vc_b, kt_b, vt_b, meta_b, q_l, kc_l, vc_l, kt_l, vt_l, meta_l,
-    weights_0, weights_1, weights_2, att, proj, keys_b, values_b, keys_l, values_l, bias_b, bias_l,
+    weights_0, weights_1, weights_2, att, proj, partial, scores, keys_b, values_b, keys_l, values_l, bias_b, bias_l,
     send_sems, recv_sems, load_sems, load_send, load_recv, w_sems, att_send, att_recv, att_sem,
     proj_send, proj_recv, proj_sem,
 ):
@@ -323,12 +371,16 @@
         for copy in message(rings, name, send_sems, recv_sems):
             copy.wait()
 
-    start("own")
+    for name in ("own", "l0", "f0"):
+        start(name)
     wait_loads(("meta", 0))
     build_bias(meta_b, bias_b, NODES, NODES)
     build_bias(meta_l, bias_l, LIGHT, LIGHT)
     count_b, count_l = meta_b[16:17, :TILE], meta_l[16:17, :TILE]
-    refs = (q_b, q_l, keys_b, values_b, keys_l, values_l, bias_b, bias_l, sinks, att)
+    refs = (q_b, q_l, keys_b, values_b, keys_l, values_l, bias_b, bias_l, sinks, att, scores)
+
+    def wide(meta):
+        return jnp.concatenate([meta[17:18, :], meta[17:18, :]], axis=1)
 
     def att_half(side, kv):
         return att.at[:, pl.ds(pl.multiple_of(side * HALF + kv * 512, 512), 512)]
@@ -356,11 +408,11 @@
             pl.when(jnp.logical_not(second))(lambda: wait_loads(("kv", pair)))
             lanes = pl.ds(pl.multiple_of(pair * 128, 128), 128)
             prepare(
-                kc_b[:, lanes], vc_b[:, lanes], kt_b[:, lanes], vt_b[:, lanes], meta_b[17:18, :],
+                kc_b[:, lanes], vc_b[:, lanes], kt_b[:, lanes], vt_b[:, lanes], wide(meta_b),
                 second, keys_b, values_b, NODES,
             )
             prepare(
-                kc_l[:, lanes], vc_l[:, lanes], kt_l[:, lanes], vt_l[:, lanes], meta_l[17:18, :],
+                kc_l[:, lanes], vc_l[:, lanes], kt_l[:, lanes], vt_l[:, lanes], wide(meta_l),
                 second, keys_l, values_l, LIGHT,
             )
 
@@ -373,11 +425,8 @@
         return carry
 
     lax.fori_loop(0, 16, per_pair, 0)
-    for name in ("back0", "back-", "back+"):
-        finish(name)
     wait_sends()
     att_swap(3).start()
-    finish("back2")
     for kv in range(4):
         att_swap(kv).wait_send()
         other = att_half(1 - core, kv)
@@ -393,12 +442,12 @@
 
     def proj_block(heavy, part):
         first, count = (0, NODES) if heavy else (NODES, LIGHT)
-        return proj.at[part, pl.ds(first, count)]
+        return proj.at[part, pl.ds(0, PART_COLS), pl.ds(first, count)]
 
     def proj_place(heavy, side, part):
         count = NODES if heavy else LIGHT
-        columns = pl.ds(pl.multiple_of(side * COLS + part * PART, PART), PART)
-        return proj_hbm.at[pl.ds(0, count), columns]
+        rows = pl.ds(pl.multiple_of((side * 3 + part) * PART_COLS, 32), PART_COLS)
+        return proj_hbm.at[rows, pl.ds(0, count)]
 
     def proj_copies(heavy, part):
         own = pltpu.make_async_copy(
@@ -422,22 +471,44 @@
         landed = proj_place(heavy, 1 - core, part)
         to_partner(landed, landed, proj_send.at[part], proj_recv.at[part]).wait_recv()
 
+    def lanes_of(rows, first, count):
+        return att[rows, pl.ds(pl.multiple_of(first, 128), count)]
+
+    def terms(part, rows, last):
+        ring = rings[part]
+        pairs = []
+        if part == 0:
+            z_hi = lax.div(place["z"], 2)
+            z_hi = 1 - z_hi if last else z_hi
+            for y in range(4):
+                pairs.append(
+                    (lanes_of(rows, (2 * y + z_hi) * 512, 512), weights_0[y, z_hi].reshape(512, PART))
+                )
+        else:
+            for by in (2,) if last else (0, 1, -1):
+                at = ring.moved(ring.order[2], by)
+                if part == 1:
+                    left = [lanes_of(rows, g * 512 + at * 128, 128) for g in range(8)]
+                    right = weights_1[:, :, at].reshape(1024, PART)
+                    pairs.append((jnp.concatenate(left, axis=1), right))
+                else:
+                    pairs.append((lanes_of(rows, at * 1024, 1024), weights_2[at].reshape(1024, PART)))
+        total = None
+        for left, right in pairs:
+            term = jnp.dot(left, right, preferred_element_type=F32)
+            total = term if total is None else total + term
+        return total
+
+    row_blocks = (pl.ds(0, 384), pl.ds(384, 256))
     for part in range(3):
-
-        def per_block(block, carry, part=part):
-            rows = pl.ds(pl.multiple_of(block * 320, 64), 320)
-            total = None
-            for gx_at in range(8):
-                term = jnp.dot(
-                    att[rows, gx_at * 512 : gx_at * 512 + 512],
-                    weights[part][gx_at // 2, gx_at % 2].reshape(512, PART),
-                    preferred_element_type=F32,
-                )
-                total = term if total is None else total + term
-            proj[part, rows, :] = total.astype(BF16)
-            return carry
-
-        lax.fori_loop(0, 2, per_block, 0)
+        for rows in row_blocks:
+            partial[part, rows, :] = terms(part, rows, False)
+    for name in ("back0", "back-", "back+", "back2"):
+        finish(name)
+    for part in range(3):
+        for rows in row_blocks:
+            total = partial[part, rows, :] + terms(part, rows, True)
+            proj[part, :, rows] = total.T.astype(BF16)
         if part > 0:
             by_role(functools.partial(start_proj, part=part - 1))
     by_role(lambda heavy: att_store(heavy).wait())
@@ -458,14 +529,14 @@
             pltpu.VMEM((CACHE, 256), BF16),
             pltpu.VMEM((rows, 256), BF16),
             pltpu.VMEM((rows, 256), BF16),
-            pltpu.VMEM((24, CACHE), jnp.int32),
+            pltpu.VMEM((24, NODES), jnp.int32),
         ]
 
     return pl.pallas_call(
         whole_kernel,
         out_shape=(
             jax.ShapeDtypeStruct((NODES, 2 * HALF), BF16),
-            jax.ShapeDtypeStruct((NODES, 2 * COLS), BF16),
+            jax.ShapeDtypeStruct((D, NODES), BF16),
         ),
         in_specs=[smem] + [hbm] * len(arrays),
         out_specs=(hbm, hbm),
@@ -474,7 +545,9 @@
         + [pltpu.VMEM((4, 2, 4, 2, 64, PART), BF16)] * 3
         + [
             pltpu.VMEM((NODES + LIGHT, 2 * HALF), BF16),
-            pltpu.VMEM((3, NODES + LIGHT, PART), BF16),
+            pltpu.VMEM((3, PART, NODES + LIGHT), BF16),
+            pltpu.VMEM((3, NODES + LIGHT, PART), F32),
+            pltpu.VMEM((2, CACHE + NODES, TILE), F32),
             pltpu.VMEM((CACHE + NODES, 128), BF16),
             pltpu.VMEM((HD + SUMS, CACHE + NODES), BF16),
             pltpu.VMEM((CACHE + LIGHT, 128), BF16),
@@ -499,22 +572,18 @@
     q_nodes, k_cache, v_cache, k_tree, v_tree, anc_bits, node_count, cache_len, sinks, o_weight
 ):
     busy = lax.rem(lax.axis_index("gx") + lax.axis_index("core"), 2) == 0
-    weight = jnp.pad(o_weight, ((0, 0), (0, 2 * COLS - D)))
-    weight = jnp.transpose(weight.reshape(32, 2, 3, PART), (1, 2, 0, 3))
-    bits = jnp.pad(anc_bits[0].T, ((0, 0), (0, CACHE - NODES)))
-    ones = jnp.ones((1, CACHE), jnp.int32)
-    meta = jnp.concatenate(
-        [bits, ones * node_count[0], ones * cache_len[0], jnp.zeros((6, CACHE), jnp.int32)], axis=0
-    )
+    weight = jnp.transpose(o_weight.reshape(32, 2, 3, PART_COLS), (1, 2, 0, 3))
+    weight = jnp.pad(weight, ((0, 0), (0, 0), (0, 0), (0, PART - PART_COLS)))
+    bits = jnp.pad(anc_bits[0].T, ((0, 8), (0, 0)))
+    row = lax.broadcasted_iota(jnp.int32, bits.shape, 0)
+    meta = jnp.where(row == 16, node_count[0], jnp.where(row == 17, cache_len[0], bits))
     attended, projected = whole(
         sinks, q_nodes[0], k_cache[0], v_cache[0], k_tree[0], v_tree[0], meta, weight
     )
-    kept = (jnp.arange(NODES) < jnp.where(busy, NODES, LIGHT))[:, None]
-
-    def place(x):
-        return jnp.where(kept, x, jnp.zeros_like(x))[None]
-
-    return place(attended), place(projected[:, :D])
+    kept = jnp.arange(NODES) < jnp.where(busy, NODES, LIGHT)
+    attended = jnp.where(kept[:, None], attended, jnp.zeros_like(attended))
+    projected = jnp.where(kept[None, :], projected, jnp.zeros_like(projected))
+    return attended[None], projected.T[None]
 
 
 def solution(mesh):

time: 109 us -> 88.2 us (0.81)
  Pallas kernels: 93.2 us -> 76 us
  local copies, waits for them, and re-layouts: 4.94 us -> 2.04 us
    pallas_call x1, Pallas kernels: 93.2 us -> 76 us  [whole(): pl.pallas_call(whole_kernel, out_shape=(jax.ShapeDtypeStruct((NODES, 2 *...]
    unnamed x1 -> x2, local copies, waits for them, and re-layouts: 2.74 us -> 0.01 us
    concatenate x1 -> x0, other arithmetic: 1.48 us -> none  [on_device(): jnp.concatenate([bits, ones * node_count[0], ones * cache_len[0], jnp.zer...]
    select_n x0 -> x1, other arithmetic: none -> 1.46 us  [on_device(): jnp.where(row == 16, node_count[0], jnp.where(row == 17, cache_len[0], bi...]
where the time goes in v4:
time: 88.2 us; the launch traced here: 88 us
  Pallas kernels  76 us (86%)
  other arithmetic  7.96 us (9%)
  local copies, waits for them, and re-layouts  2.04 us (2%)
  between operations  1.98 us (2%)
    pallas_call x1, Pallas kernels, whole(): pl.pallas_call(whole_kernel, out_shape=(jax.ShapeDtypeStruct((NODES, 2 *...  76 us
    broadcast_in_dim x2, other arithmetic, on_device(): return (attended[None], projected.T[None])  6.49 us

profile of v4, /device:TPU:1, one launch (start us, length us, event | category | flops | bytes accessed | tf_op | source)
XLA Modules:
  0.0 88.0 jit_solution(11898736286153075457)
XLA Ops:
  2.0 1.5 %select_select_fusion.meta_hbm = s32[24,512]{1,0:T(8,128)} fusion(s32[16,512]{1,0:T(8,128)} %bitcast.22, s32[]{:T(128)} %bitcast.20, s32[]{:T(128)} %bitcast.19, pred[24]{0:T(512)(128)(4,1)S(1)} %get-tuple-element.6, pred[24]{0:T(512)(128)(4,1)S(1)} %get-tuple-element.7), kind=kLoop, calls=%fused_computation.3 | loop fusion | flops 24576 | bytes 81976 | tf_op jit(solution)/shard_map/jit(_where)/select_n | solution.py:579
  3.4 1.3 %reshape.15 = bf16[32,2,3,480]{3,2,1,0:T(4,128)(2,1)S(1)} reshape(bf16[32,2880]{1,0:T(8,128)(2,1)} %param.19) | data formatting | bytes 368640 | tf_op jit(solution)/shard_map/reshape | solution.py:575
  4.7 0.1 copy.14
  4.8 0.7 pad.9.w_hbm
  5.5 76.0 %whole.1 = (bf16[512,4096]{1,0:T(8,128)(2,1)}, bf16[2880,512]{1,0:T(8,128)(2,1)}) custom-call(f32[64]{0:T(128)} %sinks.1, bf16[512,4096]{1,0:T(8,128)(2,1)} %bitcast.23, bf16[1024,512]{1,0:T(8,128)(2,1)} %bitcast.24, bf16[1024,512]{1,0:T(8,128)(2,1)} %bitcast.25, bf16[512,512]{1,0:T(8,128)(2,1)} %bitcast.26, bf16[512,512]{1,0:T(8,128)(2,1)} %bitcast.27, ...), custom_call_target="tpu_custom_call" | custom-call | flops 7650410496 | bytes 8388608 | tf_op jit(solution)/shard_map/whole/pallas_call | solution.py:535
  81.5 0.0 copy-start
  81.5 4.7 %select_bitcast_fusion = bf16[1,512,4096]{2,1,0:T(8,128)(2,1)} fusion(bf16[512,4096]{1,0:T(8,128)(2,1)} %get-tuple-element.4, pred[512]{0:T(512)(128)(4,1)S(1)} %iota_compare_fusion), kind=kLoop, calls=%fused_computation | loop fusion | flops 2097152 | bytes 8389120 | tf_op jit(solution)/shard_map/broadcast_in_dim | solution.py:586
  86.2 0.0 copy-done
  86.2 1.8 %select_bitcast_fusion.1 = bf16[1,512,2880]{1,2,0:T(8,128)(2,1)} fusion(bf16[2880,512]{1,0:T(8,128)(2,1)S(1)} %copy-done, pred[512]{0:T(512)(128)(4,1)S(1)} %iota_compare_fusion), kind=kLoop, calls=%fused_computation.1 | loop fusion | flops 1474560 | bytes 5898752 | tf_op jit(solution)/shard_map/broadcast_in_dim | solution.py:586
  (2 shorter events, 0.0 us)
Async XLA Ops:
  81.5 4.7 %copy-start = (bf16[2880,512]{1,0:T(8,128)(2,1)S(1)}, bf16[2880,512]{1,0:T(8,128)(2,1)}, u32[]{:S(2)}) copy-start(bf16[2880,512]{1,0:T(8,128)(2,1)} %get-tuple-element.5) | copy-start | bytes 8847364

commit v5 on v4

--- a/solution.py
+++ b/solution.py
@@ -10,6 +10,7 @@
 HD = 64
 NODES = 512
 LIGHT = 128
+KEEP = 4
 CACHE = 1024
 HALF = 2048
 D = 2880
@@ -23,13 +24,11 @@
 WHERE = {"x": (2,), "y": (0,), "z": (1, 3)}
 SIZES = (4, 2, 4, 2)
 PLAN = (
-    (1, ("own",), ("far", "l-", "l+", "f-", "f+")),
-    (3, ("far",), ("l2", "f2")),
-    (5, ("l0", "l-", "l+", "l2"), ("line2", "face-", "face+")),
-    (6, ("f0", "f-", "f+", "f2"), ("back0",)),
-    (7, ("line2",), ("face2",)),
-    (11, ("face-", "face+"), ("back-", "back+")),
-    (14, ("face2",), ("back2",)),
+    (1, ("far",), ("l2", "f2")),
+    (2, ("l0", "l-", "l+", "l2"), ("line2", "face-", "face+")),
+    (3, ("line2", "f0", "f-", "f+", "f2"), ("face2", "back0")),
+    (5, ("face-", "face+"), ("back-", "back+")),
+    (7, ("face2",), ("back2",)),
 )
 NAMES = (
     "own", "far", "l0", "l-", "l+", "l2", "line2", "f0", "f-", "f+", "f2", "face-", "face+",
@@ -124,49 +123,49 @@
         return self.total[:HD] * jnp.where(self.node_ok, 1.0 / denominator, 0.0)
 
 
-def attend_head_pair(pair, core, refs, counts):
+def attend_pairs(step, core, refs, counts):
     (q_busy, q_light, keys_b, values_b, keys_l, values_l, bias_b, bias_l, sinks, att, scores) = refs
     count_b, count_l = counts
-    lanes = pl.ds(pl.multiple_of(pair * 128, 128), 128)
-    out_lanes = pl.ds(pl.multiple_of(core * HALF + pair * 128, 128), 128)
-    first_head = core * 32
-    sink_even = sinks[first_head + 2 * pair] * 8.0
-    sink_odd = sinks[first_head + 2 * pair + 1] * 8.0
     columns = lane_ids((1, TILE))
-    units = []
-    for tile in range(NODES // TILE):
-        rows = pl.ds(tile * TILE, TILE)
-        for odd, sink in enumerate((sink_even, sink_odd)):
-
-            def queries(rows=rows, odd=odd):
+    units, outputs = [], {}
+    for inner in range(2):
+        pair = 2 * step + inner
+        lanes = pl.ds(pl.multiple_of(pair * 128, 128), 128)
+        out_lanes = pl.ds(pl.multiple_of(core * HALF + pair * 128, 128), 128)
+        sink_even = sinks[core * 32 + 2 * pair] * 8.0
+        sink_odd = sinks[core * 32 + 2 * pair + 1] * 8.0
+        for tile in range(NODES // TILE):
+            rows = pl.ds(tile * TILE, TILE)
+            for odd, sink in enumerate((sink_even, sink_odd)):
                 both = q_busy[rows, lanes]
-                return jnp.where((lane_ids(both.shape) < HD) == (odd == 0), both, jnp.zeros_like(both))
-
-            units.append(
-                Unit(
-                    keys_b, values_b, queries(),
-                    lambda at, count, rows=rows: bias_b[pl.ds(at, count), rows],
-                    (tile + 1) * TILE, sink, columns + tile * TILE < count_b,
-                    scores.at[len(units) % 2],
+                own = (lane_ids(both.shape) < HD) == (odd == 0)
+                units.append(
+                    Unit(
+                        keys_b, values_b, jnp.where(own, both, jnp.zeros_like(both)),
+                        lambda at, count, rows=rows: bias_b[pl.ds(at, count), rows],
+                        (tile + 1) * TILE, sink, columns + tile * TILE < count_b,
+                        scores.at[len(units) % 3],
+                    )
                 )
+            outputs[len(units) - 1] = (rows, out_lanes)
+        both = q_light[:, lanes]
+        left = lane_ids(both.shape) < HD
+        zero = jnp.zeros_like(both)
+        both = jnp.concatenate([jnp.where(left, both, zero), jnp.where(left, zero, both)], axis=0)
+        units.append(
+            Unit(
+                keys_l, values_l, both,
+                lambda at, count: jnp.concatenate([bias_l[...], bias_l[...]], axis=1), LIGHT,
+                jnp.where(columns < LIGHT, sink_even, sink_odd),
+                jnp.where(columns < LIGHT, columns, columns - LIGHT) < count_l,
+                scores.at[len(units) % 3],
             )
-    both = q_light[:, lanes]
-    left = lane_ids(both.shape) < HD
-    zero = jnp.zeros_like(both)
-    both = jnp.concatenate([jnp.where(left, both, zero), jnp.where(left, zero, both)], axis=0)
-    units.append(
-        Unit(
-            keys_l, values_l, both,
-            lambda at, count: jnp.concatenate([bias_l[...], bias_l[...]], axis=1), LIGHT,
-            jnp.where(columns < LIGHT, sink_even, sink_odd),
-            jnp.where(columns < LIGHT, columns, columns - LIGHT) < count_l,
-            scores.at[len(units) % 2],
-        )
-    )
+        )
+        outputs[len(units) - 1] = (None, out_lanes)
     results = []
-    for number in range(len(units) + 1):
+    for number in range(len(units) + 2):
         ahead = units[number] if number < len(units) else None
-        behind = units[number - 1] if number > 0 else None
+        behind = units[number - 2] if number >= 2 else None
         for chunk in range(6):
             if ahead is not None and chunk < len(ahead.chunks):
                 ahead.score(chunk)
@@ -176,12 +175,14 @@
             results.append(behind.result())
         if ahead is not None:
             ahead.settle()
-        if number in (2, 4):
-            rows = pl.ds((number // 2 - 1) * TILE, TILE)
-            att[rows, out_lanes] = jnp.concatenate(results[-2:], axis=0).T.astype(BF16)
-    result = results[-1]
-    stacked = jnp.concatenate([result[:, :LIGHT], result[:, LIGHT:]], axis=0)
-    att[pl.ds(NODES, LIGHT), out_lanes] = stacked.T.astype(BF16)
+        if number - 2 in outputs:
+            rows, out_lanes = outputs[number - 2]
+            if rows is None:
+                rows = pl.ds(NODES, LIGHT)
+                pieces = [results[-1][:, :LIGHT], results[-1][:, LIGHT:]]
+            else:
+                pieces = results[-2:]
+            att[rows, out_lanes] = jnp.concatenate(pieces, axis=0).T.astype(BF16)
 
 
 class Ring:
@@ -244,9 +245,9 @@
 
 
 def whole_kernel(
-    sinks, q_hbm, kc_hbm, vc_hbm, kt_hbm, vt_hbm, meta_hbm, w_hbm, att_hbm, proj_hbm,
+    sinks, q_hbm, kc_hbm, vc_hbm, kt_hbm, vt_hbm, bits_hbm, count_hbm, w_hbm, att_hbm, proj_hbm,
     q_b, kc_b, vc_b, kt_b, vt_b, meta_b, q_l, kc_l, vc_l, kt_l, vt_l, meta_l,
-    weights_0, weights_1, weights_2, att, proj, partial, scores, keys_b, values_b, keys_l, values_l, bias_b, bias_l,
+    weights_0, weights_1, weights_2, att, proj, partial, w_raw, w_split, scores, keys_b, values_b, keys_l, values_l, bias_b, bias_l,
     send_sems, recv_sems, load_sems, load_send, load_recv, w_sems, att_send, att_recv, att_sem,
     proj_send, proj_recv, proj_sem,
 ):
@@ -283,7 +284,7 @@
                 )
             ]
         if piece[0] == "meta":
-            return [(meta_hbm, meta)]
+            return [(bits_hbm, meta.at[pl.ds(0, 16)]), (count_hbm, meta.at[pl.ds(16, 8)])]
         source = pl.ds(half * 256 + piece[1] * 128, 128)
         target = pl.ds(pl.multiple_of(piece[1] * 128, 128), 128)
         return [
@@ -294,7 +295,7 @@
         ]
 
     def slot(piece):
-        return {"meta": 0, "q": 1, "kv": 5}[piece[0]] + piece[1] * (4 if piece[0] == "kv" else 1)
+        return {"meta": 0, "q": 2, "kv": 6}[piece[0]] + piece[1] * (4 if piece[0] == "kv" else 1)
 
     def local_loads(heavy, piece):
         pairs = load_pairs(heavy, piece, core)
@@ -334,6 +335,8 @@
 
         by_role(run)
 
+    fetch = pltpu.make_async_copy(w_hbm, w_raw, w_sems.at[3, 0])
+    fetch.start()
     barrier = pltpu.get_barrier_semaphore()
     for dim in "xyz":
         for by in (1, -1):
@@ -341,23 +344,28 @@
                 barrier, inc=1, device_id=rings[0].device(dim, by), device_id_type=MESH
             )
     pl.semaphore_signal(barrier, inc=1, device_id=partner, device_id_type=MESH)
+    fetch.wait()
+    shard = w_raw[...].astype(F32)
+    w_split[:, :, :, 384:] = jnp.zeros((2, 3, 32, PART - 384), BF16)
+    for side in range(2):
+        for part in range(3):
+            first = (side * 3 + part) * PART_COLS
+            w_split[side, part, :, :PART_COLS] = shard[:, first : first + PART_COLS].astype(BF16)
     pl.semaphore_wait(barrier, 7)
 
     rows = pl.ds(pl.multiple_of(core * 32, 32), 32)
-    chunk_local, chunk_remote = [], []
+    chunk_remote = []
     for part, ring in enumerate(rings):
         target = ring.block((0, 0, 0)).at[rows]
-        chunk_local.append(
-            pltpu.make_async_copy(w_hbm.at[core, part], target, w_sems.at[0, part])
-        )
         chunk_remote.append(
-            to_partner(w_hbm.at[1 - core, part], target, w_sems.at[1, part], w_sems.at[2, part])
-        )
-    for copy in chunk_remote + chunk_local:
+            to_partner(w_split.at[1 - core, part], target, w_sems.at[1, part], w_sems.at[2, part])
+        )
+    for copy in chunk_remote:
         copy.start()
+    for part, ring in enumerate(rings):
+        ring.block((0, 0, 0))[rows, :] = w_split[core, part]
     by_role(start_loads)
-    for local, remote, part in zip(chunk_local, chunk_remote, range(3)):
-        local.wait()
+    for part, remote in enumerate(chunk_remote):
         remote.wait_send()
         other = pl.ds(pl.multiple_of(32 - core * 32, 32), 32)
         landed = rings[part].block((0, 0, 0)).at[other]
@@ -382,15 +390,15 @@
     def wide(meta):
         return jnp.concatenate([meta[17:18, :], meta[17:18, :]], axis=1)
 
-    def att_half(side, kv):
-        return att.at[:, pl.ds(pl.multiple_of(side * HALF + kv * 512, 512), 512)]
-
-    def att_swap(kv):
-        own = att_half(core, kv)
-        return to_partner(own, own, att_send.at[kv], att_recv.at[kv])
-
-    def per_pair(step, carry):
-        kv = lax.div(step, 4)
+    def att_half(side, step):
+        return att.at[:, pl.ds(pl.multiple_of(side * HALF + step * 256, 256), 256)]
+
+    def att_swap(step):
+        own = att_half(core, step)
+        return to_partner(own, own, att_send.at[step], att_recv.at[step])
+
+    def per_step(step, carry):
+        kv = lax.div(step, 2)
         for when, waits, starts in PLAN:
 
             @pl.when(step == when)
@@ -400,7 +408,7 @@
                 for name in starts:
                     start(name)
 
-        @pl.when(lax.rem(step, 4) == 0)
+        @pl.when(lax.rem(step, 2) == 0)
         def _():
             pair = lax.div(kv, 2)
             second = lax.rem(kv, 2) == 1
@@ -416,21 +424,23 @@
                 second, keys_l, values_l, LIGHT,
             )
 
-        attend_head_pair(step, core, refs, (count_b, count_l))
-
-        @pl.when((lax.rem(step, 4) == 0) & (step > 0))
+        @pl.when(step == 0)
         def _():
-            att_swap(kv - 1).start()
-
+            finish("own")
+            for name in ("far", "l-", "l+", "f-", "f+"):
+                start(name)
+
+        attend_pairs(step, core, refs, (count_b, count_l))
+        pl.when(step > 0)(lambda: att_swap(step - 1).start())
         return carry
 
-    lax.fori_loop(0, 16, per_pair, 0)
+    lax.fori_loop(0, 8, per_step, 0)
     wait_sends()
-    att_swap(3).start()
-    for kv in range(4):
-        att_swap(kv).wait_send()
-        other = att_half(1 - core, kv)
-        to_partner(other, other, att_send.at[kv], att_recv.at[kv]).wait_recv()
+    att_swap(7).start()
+    for step in range(8):
+        att_swap(step).wait_send()
+        other = att_half(1 - core, step)
+        to_partner(other, other, att_send.at[step], att_recv.at[step]).wait_recv()
 
     def att_store(heavy):
         first, count = (0, NODES) if heavy else (NODES, LIGHT)
@@ -547,7 +557,9 @@
             pltpu.VMEM((NODES + LIGHT, 2 * HALF), BF16),
             pltpu.VMEM((3, PART, NODES + LIGHT), BF16),
             pltpu.VMEM((3, NODES + LIGHT, PART), F32),
-            pltpu.VMEM((2, CACHE + NODES, TILE), F32),
+            pltpu.VMEM((32, D), BF16),
+            pltpu.VMEM((2, 3, 32, PART), BF16),
+            pltpu.VMEM((3, CACHE + NODES, TILE), F32),
             pltpu.VMEM((CACHE + NODES, 128), BF16),
             pltpu.VMEM((HD + SUMS, CACHE + NODES), BF16),
             pltpu.VMEM((CACHE + LIGHT, 128), BF16),
@@ -555,8 +567,8 @@
             pltpu.VMEM((NODES, NODES), F32),
             pltpu.VMEM((LIGHT, LIGHT), F32),
             dma((len(NAMES), 3, 2)), dma((len(NAMES), 3, 2)),
-            dma((13,)), dma((13,)), dma((13,)), dma((3, 3)),
-            dma((4,)), dma((4,)), dma, dma((3,)), dma((3,)), dma((3,)),
+            dma((14,)), dma((14,)), dma((14,)), dma((4, 3)),
+            dma((8,)), dma((8,)), dma, dma((3,)), dma((3,)), dma((3,)),
         ],
         compiler_params=pltpu.CompilerParams(
             vmem_limit_bytes=60 * 1024 * 1024, collective_id=0, has_side_effects=True
@@ -568,21 +580,64 @@
     )(sinks, *arrays)
 
 
+def keep_kernel(limit, att_in, proj_in, att_out, proj_out, att, proj, in_sems, out_sems):
+    att_rows, proj_rows = NODES // KEEP, D // KEEP
+    moves = []
+    for i in range(KEEP):
+        rows = pl.ds(i * att_rows, att_rows)
+        moves.append((att_in.at[rows], att.at[rows], att_out.at[rows], rows))
+        rows = pl.ds(i * proj_rows, proj_rows)
+        moves.append((proj_in.at[rows], proj.at[rows], proj_out.at[rows], rows))
+    reads = [pltpu.make_async_copy(m[0], m[1], in_sems.at[i]) for i, m in enumerate(moves)]
+    writes = [pltpu.make_async_copy(m[1], m[2], out_sems.at[i]) for i, m in enumerate(moves)]
+    for copy in reads:
+        copy.start()
+    for i, move in enumerate(moves):
+        reads[i].wait()
+
+        @pl.when(limit[0] < NODES)
+        def _():
+            if i % 2 == 0:
+                if i // 2 * att_rows >= LIGHT:
+                    att[move[3], :] = jnp.zeros((att_rows, 2 * HALF), BF16)
+            else:
+                proj[move[3], LIGHT:] = jnp.zeros((proj_rows, NODES - LIGHT), BF16)
+
+        writes[i].start()
+    for copy in writes:
+        copy.wait()
+
+
+def keep_live(limit, attended, projected):
+    hbm = pl.BlockSpec(memory_space=pl.ANY)
+    dma = pltpu.SemaphoreType.DMA
+    return pl.pallas_call(
+        keep_kernel,
+        out_shape=(
+            jax.ShapeDtypeStruct(attended.shape, BF16), jax.ShapeDtypeStruct(projected.shape, BF16)
+        ),
+        in_specs=[pl.BlockSpec(memory_space=pltpu.SMEM), hbm, hbm],
+        out_specs=(hbm, hbm),
+        scratch_shapes=[
+            pltpu.VMEM(attended.shape, BF16), pltpu.VMEM(projected.shape, BF16),
+            dma((2 * KEEP,)), dma((2 * KEEP,)),
+        ],
+        compiler_params=pltpu.CompilerParams(vmem_limit_bytes=60 * 1024 * 1024),
+        name="keep",
+    )(limit, attended, projected)
+
+
 def on_device(
     q_nodes, k_cache, v_cache, k_tree, v_tree, anc_bits, node_count, cache_len, sinks, o_weight
 ):
     busy = lax.rem(lax.axis_index("gx") + lax.axis_index("core"), 2) == 0
-    weight = jnp.transpose(o_weight.reshape(32, 2, 3, PART_COLS), (1, 2, 0, 3))
-    weight = jnp.pad(weight, ((0, 0), (0, 0), (0, 0), (0, PART - PART_COLS)))
-    bits = jnp.pad(anc_bits[0].T, ((0, 8), (0, 0)))
-    row = lax.broadcasted_iota(jnp.int32, bits.shape, 0)
-    meta = jnp.where(row == 16, node_count[0], jnp.where(row == 17, cache_len[0], bits))
+    row = lax.broadcasted_iota(jnp.int32, (8, NODES), 0)
+    counts = jnp.where(row == 0, node_count[0], cache_len[0])
     attended, projected = whole(
-        sinks, q_nodes[0], k_cache[0], v_cache[0], k_tree[0], v_tree[0], meta, weight
+        sinks, q_nodes[0], k_cache[0], v_cache[0], k_tree[0], v_tree[0], anc_bits[0].T, counts, o_weight
     )
-    kept = jnp.arange(NODES) < jnp.where(busy, NODES, LIGHT)
-    attended = jnp.where(kept[:, None], attended, jnp.zeros_like(attended))
-    projected = jnp.where(kept[None, :], projected, jnp.zeros_like(projected))
+    limit = jnp.where(busy, NODES, LIGHT).astype(jnp.int32)[None]
+    attended, projected = keep_live(limit, attended, projected)
     return attended[None], projected.T[None]
 
 

time: 88.2 us -> 80.5 us (0.913)
  other arithmetic: 7.96 us -> 0.01 us
  Pallas kernels: 76 us -> 77.7 us
  local copies, waits for them, and re-layouts: 2.04 us -> 0.67 us
    broadcast_in_dim x2 -> x0, other arithmetic: 6.49 us -> none  [on_device(): return (attended[None], projected.T[None])]
    pallas_call x0 -> x1, Pallas kernels: none -> 5.99 us  [keep_live(): pl.pallas_call(keep_kernel, out_shape=(jax.ShapeDtypeStruct(attended.shap...]
    pallas_call x1, Pallas kernels: 76 us -> 71.7 us  [whole(): pl.pallas_call(whole_kernel, out_shape=(jax.ShapeDtypeStruct((NODES, 2 *...]
    select_n x1, other arithmetic: 1.46 us -> 0.01 us  [on_device(): counts = jnp.where(row == 0, node_count[0], cache_len[0])]
    reshape x2 -> x0, local copies, waits for them, and re-layouts: 1.34 us -> none  [on_device(): weight = jnp.transpose(o_weight.reshape(32, 2, 3, PART_COLS), (1, 2, 0, 3))]
where the time goes in v5:
time: 80.5 us; the launch traced here: 80.3 us
  Pallas kernels  77.7 us (97%)
  between operations  1.95 us (2%)
    pallas_call x1, Pallas kernels, whole(): pl.pallas_call(whole_kernel, out_shape=(jax.ShapeDtypeStruct((NODES, 2 *...  71.7 us
    pallas_call x1, Pallas kernels, keep_live(): pl.pallas_call(keep_kernel, out_shape=(jax.ShapeDtypeStruct(attended.shap...  5.99 us

profile of v5, /device:TPU:1, one launch (start us, length us, event | category | flops | bytes accessed | tf_op | source)
XLA Modules:
  0.0 80.3 jit_solution(6760689039708664812)
XLA Ops:
  1.9 0.7 iota.7.count_hbm
  2.6 71.7 %whole.1 = (bf16[512,4096]{1,0:T(8,128)(2,1)}, bf16[2880,512]{1,0:T(8,128)(2,1)}) custom-call(f32[64]{0:T(128)} %sinks.1, bf16[512,4096]{1,0:T(8,128)(2,1)} %bitcast.17, bf16[1024,512]{1,0:T(8,128)(2,1)} %bitcast.20, bf16[1024,512]{1,0:T(8,128)(2,1)} %bitcast.21, bf16[512,512]{1,0:T(8,128)(2,1)} %bitcast.22, bf16[512,512]{1,0:T(8,128)(2,1)} %bitcast.23, ...), custom_call_target="tpu_custom_call" | custom-call | flops 7650410496 | bytes 8388608 | tf_op jit(solution)/shard_map/whole/pallas_call | solution.py:545
  74.3 6.0 %keep.1 = (bf16[512,4096]{1,0:T(8,128)(2,1)}, bf16[2880,512]{1,0:T(8,128)(2,1)}) custom-call(s32[1]{0:T(128)} %bitcast.limit, bf16[512,4096]{1,0:T(8,128)(2,1)} %get-tuple-element.6.att_in, bf16[2880,512]{1,0:T(8,128)(2,1)} %get-tuple-element.7.proj_in), custom_call_target="tpu_custom_call" | custom-call | tf_op jit(solution)/shard_map/keep/pallas_call | solution.py:614
  (1 shorter events, 0.0 us)

commit v6 on v5

--- a/solution.py
+++ b/solution.py
@@ -27,8 +27,7 @@
     (1, ("far",), ("l2", "f2")),
     (2, ("l0", "l-", "l+", "l2"), ("line2", "face-", "face+")),
     (3, ("line2", "f0", "f-", "f+", "f2"), ("face2", "back0")),
-    (5, ("face-", "face+"), ("back-", "back+")),
-    (7, ("face2",), ("back2",)),
+    (6, ("face-", "face+"), ("back-", "back+")),
 )
 NAMES = (
     "own", "far", "l0", "l-", "l+", "l2", "line2", "f0", "f-", "f+", "f2", "face-", "face+",
@@ -437,6 +436,8 @@
     lax.fori_loop(0, 8, per_step, 0)
     wait_sends()
     att_swap(7).start()
+    finish("face2")
+    start("back2")
     for step in range(8):
         att_swap(step).wait_send()
         other = att_half(1 - core, step)

time: 80.5 us -> 78.9 us (0.980)
  Pallas kernels: 77.7 us -> 76.1 us
    pallas_call x1, Pallas kernels: 71.7 us -> 70.2 us  [whole(): pl.pallas_call(whole_kernel, out_shape=(jax.ShapeDtypeStruct((NODES, 2 *...]
where the time goes in v6:
time: 78.9 us; the launch traced here: 78.8 us
  Pallas kernels  76.1 us (96%)
  between operations  1.95 us (2%)
    pallas_call x1, Pallas kernels, whole(): pl.pallas_call(whole_kernel, out_shape=(jax.ShapeDtypeStruct((NODES, 2 *...  70.2 us
    pallas_call x1, Pallas kernels, keep_live(): pl.pallas_call(keep_kernel, out_shape=(jax.ShapeDtypeStruct(attended.shap...  5.99 us

profile of v6, /device:TPU:1, one launch (start us, length us, event | category | flops | bytes accessed | tf_op | source)
XLA Modules:
  0.0 78.8 jit_solution(4234452222606615585)
XLA Ops:
  1.9 0.7 iota.7.count_hbm
  2.6 70.2 %whole.1 = (bf16[512,4096]{1,0:T(8,128)(2,1)}, bf16[2880,512]{1,0:T(8,128)(2,1)}) custom-call(f32[64]{0:T(128)} %sinks.1, bf16[512,4096]{1,0:T(8,128)(2,1)} %bitcast.17, bf16[1024,512]{1,0:T(8,128)(2,1)} %bitcast.20, bf16[1024,512]{1,0:T(8,128)(2,1)} %bitcast.21, bf16[512,512]{1,0:T(8,128)(2,1)} %bitcast.22, bf16[512,512]{1,0:T(8,128)(2,1)} %bitcast.23, ...), custom_call_target="tpu_custom_call" | custom-call | flops 7650410496 | bytes 8388608 | tf_op jit(solution)/shard_map/whole/pallas_call | solution.py:546
  72.8 6.0 %keep.1 = (bf16[512,4096]{1,0:T(8,128)(2,1)}, bf16[2880,512]{1,0:T(8,128)(2,1)}) custom-call(s32[1]{0:T(128)} %bitcast.limit, bf16[512,4096]{1,0:T(8,128)(2,1)} %get-tuple-element.6.att_in, bf16[2880,512]{1,0:T(8,128)(2,1)} %get-tuple-element.7.proj_in), custom_call_target="tpu_custom_call" | custom-call | tf_op jit(solution)/shard_map/keep/pallas_call | solution.py:615
  (1 shorter events, 0.0 us)
